TPU v7x, 32 devices: a whole 2x2x4 slice. The times are simulated.
32 devices in a mesh: seq: 8 (over z, x), head: 4 (over y, core).
Axes of the slice: x: 2, y: 2, z: 4, core: 2. Of those that a mesh axis runs over, the one named last changes fastest.
Arguments:
- query_in: bfloat16 [2048, 8192], P('seq', 'head'), may hold values from -1.796875 to 1.796875
- key_in: bfloat16 [2048, 8192], P('seq', 'head'), may hold values from -1.796875 to 1.796875
- value_in: bfloat16 [2048, 8192], P('seq', 'head'), may hold values from -11 to 11
- log_decay: float32 [2048, 64], P('seq', 'head'), may hold values from -1 to 0, as said below
- norm_gain: float32 [8192], P('head'), may hold values from 0.5 to 1.5
- prompt_lengths: int32 [4], replicated, may hold values from 1 to 1536, 2048 in all
- step_query: bfloat16 [4, 128, 8192], P(None, 'seq', 'head'), may hold values from -1.796875 to 1.796875
- step_key: bfloat16 [4, 128, 8192], P(None, 'seq', 'head'), may hold values from -1.796875 to 1.796875
- step_value: bfloat16 [4, 128, 8192], P(None, 'seq', 'head'), may hold values from -6 to 6
- step_decay: float32 [4, 128, 64], P(None, 'seq', 'head'), may hold values from -0.3 to -0.01
- row_prompt: int32 [128], P('seq'), may hold values from 0 to 3
Outputs:
- attn_out: bfloat16 [2048, 8192], P('seq', 'head')
- decode_out: bfloat16 [4, 128, 8192], P(None, 'seq', 'head')
Inputs may be any that keep to these rules, and one draw needn't show every extreme that they name: `log_decay`: Negative; per head and token.
All inputs are finite; a program needn't handle non-finite values.
Results may differ from a plain program's by a relative error of at most 0.0056.
Values sent between devices are 32-bit elements; how exact they have to be, the bound alone decides.
A program may use at most 64 MiB of HBM per device.

v0:
```python
import jax
import jax.numpy as jnp
from jax import lax
from jax.sharding import PartitionSpec as P

HEAD_COUNT = 64
HDIM = 128
BLOCK = 256
PROMPTS = 4


EPSILON = 1e-06


def carried_in(part, axis, combine, identity):
    place = lax.axis_index(axis)
    gathered = jax.tree.map(lambda a: lax.all_gather(a, axis), part)
    state = jax.tree.map(lambda a, e: jnp.zeros_like(a) + jnp.asarray(e, a.dtype), part, identity)

    def one(step, state):
        return combine(
            state, jax.tree.map(lambda a: lax.dynamic_index_in_dim(a, step, 0, False), gathered)
        )

    return lax.fori_loop(0, place, one, state)


def segment_ids(prompt_lengths, positions):
    boundary = jnp.cumsum(prompt_lengths)
    return jnp.sum((positions[:, None] >= boundary[None, :]).astype(jnp.int32), axis=1)


def combine_pairs(earlier, later):
    return (earlier[0] * later[0], later[0][:, None, None] * earlier[1] + later[1])


def local(
    query_in,
    key_in,
    value_in,
    log_decay,
    norm_gain,
    prompt_lengths,
    step_query,
    step_key,
    step_value,
    step_decay,
    row_prompt,
):
    tok_count = query_in.shape[0]
    heads_here = log_decay.shape[1]
    nblocks = tok_count // BLOCK
    first = lax.axis_index("seq") * tok_count
    positions = first + jnp.arange(tok_count, dtype=jnp.int32)
    segs = segment_ids(prompt_lengths, positions)
    seg_entry = jnp.where(first > 0, segment_ids(prompt_lengths, (first - 1)[None])[0], -1)
    shape4 = (nblocks, BLOCK, heads_here, HDIM)
    queries = query_in.reshape(shape4)
    keys_blk = key_in.reshape(shape4)
    values_blk = value_in.reshape(shape4)
    cumul = jnp.cumsum(log_decay.reshape(nblocks, BLOCK, heads_here), axis=1)
    seg_blocks = segs.reshape(nblocks, BLOCK)
    seg_front = jnp.concatenate([seg_entry[None], seg_blocks[:-1, -1]])
    causal = jnp.arange(BLOCK)[:, None] >= jnp.arange(BLOCK)[None, :]
    linked = (causal[None] & (seg_blocks[:, :, None] == seg_blocks[:, None, :]))[:, None]
    cum_heads = jnp.transpose(cumul, (0, 2, 1))
    spread = cum_heads[:, :, :, None] - cum_heads[:, :, None, :]
    factor = jnp.where(linked, jnp.exp(jnp.where(linked, spread, 0.0)), 0.0)
    scores = jnp.einsum("nthd,nshd->nhts", queries, keys_blk, preferred_element_type=jnp.float32)
    weights = (scores * factor).astype(jnp.bfloat16)
    inner = jnp.einsum("nhts,nshd->nthd", weights, values_blk, preferred_element_type=jnp.float32)
    keep = (
        jnp.exp(cumul[:, -1:, :] - cumul)
        * (seg_blocks == seg_blocks[:, -1:]).astype(jnp.float32)[:, :, None]
    )
    keyed = (keys_blk.astype(jnp.float32) * keep[..., None]).astype(jnp.bfloat16)
    updates = jnp.einsum("nshd,nshe->nhde", keyed, values_blk, preferred_element_type=jnp.float32)
    onward = (
        jnp.exp(cumul[:, -1, :]) * (seg_blocks[:, -1] == seg_front).astype(jnp.float32)[:, None]
    )
    local_states = [jnp.zeros((heads_here, HDIM, HDIM), jnp.float32)]
    growth = [jnp.ones((heads_here,), jnp.float32)]
    blk_index = 0
    local_states.append(onward[blk_index][:, None, None] * local_states[-1] + updates[blk_index])
    growth.append(onward[blk_index] * growth[-1])
    summary = (growth[-1], local_states[-1])
    identity = (
        jnp.ones((heads_here,), jnp.float32),
        jnp.zeros((heads_here, HDIM, HDIM), jnp.float32),
    )
    entry = carried_in(summary, "seq", combine_pairs, identity)
    entry_state = entry[1]
    start_states = jnp.stack([local_states[0] + growth[0][:, None, None] * entry_state])
    state_half = start_states.astype(jnp.bfloat16)
    carried = jnp.exp(cumul) * (seg_blocks == seg_front[:, None]).astype(jnp.float32)[:, :, None]
    outer = (
        jnp.einsum("nthd,nhde->nthe", queries, state_half, preferred_element_type=jnp.float32)
        * carried[..., None]
    )
    mixed = (inner + outer).reshape(tok_count, heads_here * HDIM)
    squares = lax.psum(jnp.sum(mixed * mixed, axis=1), "head")
    scale = lax.rsqrt(squares / (HEAD_COUNT * HDIM) + EPSILON)
    attn_out = (mixed * scale[:, None] * norm_gain[None, :]).astype(jnp.bfloat16)
    boundary = jnp.cumsum(prompt_lengths)

    def prompt_end(prompt):
        last_tok = boundary[prompt] - 1
        local_tok = last_tok - first
        owned = (local_tok >= 0) & (local_tok < tok_count)
        safe_tok = jnp.clip(local_tok, 0, tok_count - 1)
        blk_index = safe_tok // BLOCK
        offset = safe_tok - blk_index * BLOCK
        cum_blk = cumul[blk_index]
        reached = cum_blk[offset]
        taken = (jnp.arange(BLOCK) <= offset) & (seg_blocks[blk_index] == prompt)
        keep_end = (
            jnp.exp(jnp.where(taken[:, None], reached[None, :] - cum_blk, 0.0))
            * taken.astype(jnp.float32)[:, None]
        )
        tailed = (keys_blk[blk_index].astype(jnp.float32) * keep_end[:, :, None]).astype(
            jnp.bfloat16
        )
        part = jnp.einsum(
            "shd,she->hde", tailed, values_blk[blk_index], preferred_element_type=jnp.float32
        )
        lead = jnp.exp(reached) * (seg_front[blk_index] == prompt).astype(jnp.float32)
        total = lead[:, None, None] * start_states[blk_index] + part
        return total * owned.astype(jnp.float32)

    candidates = lax.map(prompt_end, jnp.arange(PROMPTS, dtype=jnp.int32))
    prompt_state = lax.psum(candidates, "seq")
    rows_here = row_prompt.shape[0]
    row_states = jnp.take(prompt_state, row_prompt, axis=0)
    results = []
    for section in range(step_query.shape[0]):
        query_now = step_query[section].astype(jnp.float32).reshape(rows_here, heads_here, HDIM)
        key_now = step_key[section].astype(jnp.float32).reshape(rows_here, heads_here, HDIM)
        value_now = step_value[section].astype(jnp.float32).reshape(rows_here, heads_here, HDIM)
        row_states = (
            jnp.exp(step_decay[section])[:, :, None, None] * row_states
            + key_now[:, :, :, None] * value_now[:, :, None, :]
        )
        results.append(
            jnp.einsum(
                "rhd,rhde->rhe", query_now, row_states, precision=lax.Precision.HIGHEST
            ).reshape(rows_here, heads_here * HDIM)
        )
    decoded = jnp.stack(results)
    step_squares = lax.psum(jnp.sum(decoded * decoded, axis=2), "head")
    step_scale = lax.rsqrt(step_squares / (HEAD_COUNT * HDIM) + EPSILON)
    decode_out = (decoded * step_scale[:, :, None] * norm_gain[None, None, :]).astype(jnp.bfloat16)
    return (attn_out, decode_out)


def solution(mesh):
    in_specs = (
        P("seq", "head"),
        P("seq", "head"),
        P("seq", "head"),
        P("seq", "head"),
        P("head"),
        P(),
        P(None, "seq", "head"),
        P(None, "seq", "head"),
        P(None, "seq", "head"),
        P(None, "seq", "head"),
        P("seq"),
    )
    out_specs = (P("seq", "head"), P(None, "seq", "head"))
    return jax.shard_map(local, mesh=mesh, in_specs=in_specs, out_specs=out_specs, check_vma=False)
```

profile of v0, /device:TPU:0, one launch (start us, length us, event | category | flops | bytes accessed | tf_op | source)
XLA Modules:
  0.0 465.5 jit_solution(464305001508278530)
XLA Ops:
  14.8 2.6 convolution_add_fusion.1
  20.5 22.7 %all-gather = f32[8,1,16]{2,1,0:T(1,128)S(1)} all-gather(f32[1,1,16]{2,1,0:T(1,128)S(1)} %get-tuple-element.344), channel_id=2, replica_groups=mesh['seq'=8,'head'=4] {'seq'}, dimensions={0}, use_global_device_ids=true | all-gather | bytes 576 | tf_op jit(solution)/shard_map/all_gather | solution.py:17
  43.2 101.7 %all-gather.4.cloned.1.call-done = f32[128,128,128]{2,1,0:T(8,128)} async-done(((f32[16,128,128]{2,1,0:T(8,128)}), f32[128,128,128]{2,1,0:T(8,128)}) %all-gather.4.cloned.1.call-update) | async-done | bytes 8388624 | tf_op jit(solution)/shard_map/all_gather | solution.py:17
  145.0 32.4 %while.26 = (s32[]{:T(128)}, f32[4,16,128,128]{3,2,1,0:T(8,128)}, s32[4]{0:T(128)S(1)}, s32[4]{0:T(128)S(1)}, s32[]{:T(128)}, /*index=5*/f32[1,256,16]{1,2,0:T(8...) while((s32[]{:T(128)}, f32[4,16,128,128]{3,2,1,0:T(8,128)}, ...), condition=%wide.region_10.11_spmd, body=%wide.region_9.10_spmd.sunk | while | flops 136590384 | bytes 4248923 | solution.py:130
  150.4 2.7 fusion.78
  158.6 2.6 fusion.78
  166.7 2.7 fusion.78
  174.7 2.6 fusion.78
  177.4 1.6 convert_bitcast_fusion.1
  179.7 1.7 convert_bitcast_fusion
  183.4 1.6 fusion.54
  186.6 1.6 reshape.534
  191.4 1.6 reshape.538
  198.2 4.4 fusion.36
  202.6 4.1 multiply_reduce_fusion
  206.7 1.9 copy.131
  208.7 133.8 %all-reduce.3.cloned.1.call-done = f32[4,16,128,128]{3,2,1,0:T(8,128)} async-done(((f32[4,16,128,128]{3,2,1,0:T(8,128)}), f32[4,16,128,128]{3,2,1,0:T(8,128)}) %all-reduce.3.cloned.1.call-update) | async-done | bytes 4194320 | tf_op jit(solution)/shard_map/psum | solution.py:131
  342.5 10.2 %gather_fusion = f32[16,16,128,128]{3,2,1,0:T(8,128)} fusion(f32[4,16,128,128]{3,2,1,0:T(8,128)} %all-reduce.3.cloned.1.call-done, s32[1024]{0:T(1024)S(1)} %pad_clamp_fusion), kind=kCustom, calls=%fused_computation | custom fusion | bytes 33554496 | tf_op jit(solution)/shard_map/jit(_take)/gather | solution.py:133
  352.7 17.9 %fusion.15 = f32[16,16,1,128]{3,2,1,0:T(1,128)} fusion(bf16[16,16,128,1]{2,3,1,0:T(2,128)(2,1)S(1)} %copy-done.3, f32[16,16,128]{2,1,0:T(8,128)} %bitcast.215, f32[16,16,128]{2,1,0:T(8,128)} %bitcast.212, f32[16,16]{1,0:T(8,128)S(1)} %get-tuple-element.346, f32[16,16,128,128]{3,2,1,0:T(8,128)} %gather_fusion, f32[16,16,128]{2,1,0:T(8,128)} %bitcast.208, ...), kind=kOutput, calls=%fused_computation.28 | convolution fusion | flops 79691776 | bytes 17500176 | tf_op jit(solution)/shard_map/rhd,rhde->rhe/dot_general | solution.py:144
  371.6 13.4 %fusion.52 = f32[16,16,1,128]{3,2,1,0:T(1,128)} fusion(bf16[16,16,128,1]{2,3,1,0:T(2,128)(2,1)S(1)} %copy-done.2, f32[16,16,128,128]{3,2,1,0:T(8,128)} %gather_fusion, f32[16,16,128]{2,1,0:T(8,128)} %bitcast.209, f32[16,16,128]{2,1,0:T(8,128)S(1)} %bitcast.207, f32[16,16]{1,0:T(8,128)} %get-tuple-element.347, pred[16]{0:T(512)(128)(4,1)} %compare_and_fusion.1), kind=kOutput, calls=%fused_computation.108 | convolution fusion | flops 67108864 | bytes 17237008 | tf_op jit(solution)/shard_map/rhd,rhde->rhe/dot_general | solution.py:144
  386.6 22.6 %fusion.16 = f32[16,16,1,128]{3,2,1,0:T(1,128)} fusion(bf16[16,16,128,1]{2,3,1,0:T(2,128)(2,1)} %reshape.538, f32[16,16,128]{2,1,0:T(8,128)} %bitcast.220, f32[16,16,128]{2,1,0:T(8,128)} %bitcast.218, f32[16,16]{1,0:T(8,128)} %get-tuple-element.348, f32[16,16,128]{2,1,0:T(8,128)} %bitcast.216, f32[16,16,128]{2,1,0:T(8,128)} %bitcast.213, ...), kind=kOutput, calls=%fused_computation.29 | convolution fusion | flops 92274688 | bytes 17763344 | tf_op jit(solution)/shard_map/rhd,rhde->rhe/dot_general | solution.py:144
  410.1 34.9 %fusion.11 = f32[16,16,1,128]{3,2,1,0:T(1,128)} fusion(bf16[16,16,128,1]{2,3,1,0:T(2,128)(2,1)S(1)} %copy-done.1, f32[16,16,128]{2,1,0:T(8,128)} %bitcast.223, f32[16,16,128]{2,1,0:T(8,128)} %bitcast.222, f32[16,16]{1,0:T(8,128)S(1)} %get-tuple-element.345, f32[16,16,128]{2,1,0:T(8,128)} %bitcast.221, f32[16,16,128]{2,1,0:T(8,128)} %bitcast.219, ...), kind=kOutput, calls=%fused_computation.21 | convolution fusion | flops 104857600 | bytes 18026512 | tf_op jit(solution)/shard_map/rhd,rhde->rhe/dot_general | solution.py:144
  449.1 6.4 %all-reduce = (f32[256]{0:T(256)S(1)}, f32[4,16]{1,0:T(4,128)S(1)}) all-reduce(f32[256]{0:T(256)} %get-tuple-element.351, f32[4,16]{1,0:T(4,128)S(1)} %multiply_reduce_fusion.1), channel_id=1, replica_groups=mesh['seq'=8,'head'=4] {'head'}, use_global_device_ids=true, to_apply=%region_8.9 | all-reduce | flops 320 | bytes 2560 | tf_op jit(solution)/shard_map/psum | solution.py:101
  455.6 1.9 multiply_convert_fusion.4
  (106 shorter events, 39.3 us)
Async XLA Ops:
  7.2 191.1 %copy-start = (bf16[256,2048]{1,0:T(8,128)(2,1)S(1)}, bf16[256,2048]{1,0:T(8,128)(2,1)}, u32[]{:S(2)}) copy-start(bf16[256,2048]{1,0:T(8,128)(2,1)} %param.15) | copy-start | bytes 3145732
  7.2 137.7 %all-gather.4.cloned.1.call-start = ((), (), s32[]{:S(2)}) async-start(), calls=%async_computation.1 | async-start | bytes 9437184 | tf_op jit(solution)/shard_map/all_gather | solution.py:17
  17.5 325.0 %all-reduce.3.cloned.1.call-start = ((), (), s32[]{:S(2)}) async-start(), calls=%async_computation | async-start | bytes 8388608 | tf_op jit(solution)/shard_map/psum | solution.py:131
  145.0 51.2 %copy-start.7 = (s32[16]{0:T(128)S(1)}, s32[16]{0:T(128)}, u32[]{:S(2)}) copy-start(s32[16]{0:T(128)} %param.25) | copy-start | bytes 196
  198.1 188.4 %copy-start.6 = (f32[16,16]{1,0:T(8,128)}, f32[16,16]{1,0:T(8,128)S(1)}, u32[]{:S(2)}) copy-start(f32[16,16]{1,0:T(8,128)S(1)} %get-tuple-element.346) | copy-start | bytes 3076
  208.6 144.1 %copy-start.3 = (bf16[16,16,128,1]{2,3,1,0:T(2,128)(2,1)S(1)}, bf16[16,16,128,1]{2,3,1,0:T(2,128)(2,1)}, u32[]{:S(2)}) copy-start(bf16[16,16,128,1]{2,3,1,0:T(2,128)(2,1)} %reshape.536) | copy-start | bytes 196612
  208.7 144.1 %copy-start.4 = (f32[2,8,16,128]{3,2,1,0:T(8,128)S(1)}, f32[2,8,16,128]{3,2,1,0:T(8,128)}, u32[]{:S(2)}) copy-start(f32[2,8,16,128]{3,2,1,0:T(8,128)} %copy.151) | copy-start | bytes 393220
  352.7 18.9 %copy-start.2 = (bf16[16,16,128,1]{2,3,1,0:T(2,128)(2,1)S(1)}, bf16[16,16,128,1]{2,3,1,0:T(2,128)(2,1)}, u32[]{:S(2)}) copy-start(bf16[16,16,128,1]{2,3,1,0:T(2,128)(2,1)} %reshape.534) | copy-start | bytes 196612
  386.6 23.6 %copy-start.1 = (bf16[16,16,128,1]{2,3,1,0:T(2,128)(2,1)S(1)}, bf16[16,16,128,1]{2,3,1,0:T(2,128)(2,1)}, u32[]{:S(2)}) copy-start(bf16[16,16,128,1]{2,3,1,0:T(2,128)(2,1)} %reshape.540) | copy-start | bytes 196612
  410.1 45.4 %copy-start.5 = (f32[2048]{0:T(1024)S(1)}, f32[2048]{0:T(1024)}, u32[]{:S(2)}) copy-start(f32[2048]{0:T(1024)} %param.19) | copy-start | bytes 24580
Sparse Core Ops, SparseCore 0:
  17.6 127.2 all-gather.3
  177.5 164.8 all-reduce.2
where the time goes:
time: 467 us; the launch traced here: 465 us
  waiting for transfers between devices  235 us (50%)
  matrix products  111 us (24%)
  local copies, waits for them, and re-layouts  47 us (10%)
  blocking collectives  29.1 us (6%)
  between operations  15.6 us (3%)
  other arithmetic  14.4 us (3%)
  loops' own time  13.2 us (3%)
    psum x1, waiting for transfers between devices, local(): prompt_state = lax.psum(candidates, 'seq')  134 us
    all_gather x1, waiting for transfers between devices, carried_in(): gathered = jax.tree.map(lambda a: lax.all_gather(a, axis), part)  102 us
    dot_general x4, matrix products, local(): jnp.einsum('rhd,rhde->rhe', query_now, row_states, precision=lax.Precisio...  88.8 us
    all_gather x1, blocking collectives, carried_in(): gathered = jax.tree.map(lambda a: lax.all_gather(a, axis), part)  22.7 us
    another operation x1, loops' own time, local(): candidates = lax.map(prompt_end, jnp.arange(PROMPTS, dtype=jnp.int32))  13.2 us
    unnamed x28, local copies, waits for them, and re-layouts  11.6 us
    dot_general x4, matrix products, prompt_end(): jnp.einsum('shd,she->hde', tailed, values_blk[blk_index], preferred_eleme...  10.7 us
    gather x1, local copies, waits for them, and re-layouts, local(): row_states = jnp.take(prompt_state, row_prompt, axis=0)  10.2 us
  transfers between devices with their start and end apart: 2, of which 2 were waited for; matrix products, arithmetic and copies ran while one was open for 7% of the time, Pallas kernels for 0%

commit v1 on v0

v1 whole, which is shorter than its diff:
```python
import functools

import jax
import jax.numpy as jnp
from jax import lax
from jax.experimental import pallas as pl
from jax.experimental.pallas import tpu as pltpu
from jax.sharding import PartitionSpec as P

HEAD_COUNT = 64
HDIM = 128
BLOCK = 256
PROMPTS = 4
PAIR = 2


EPSILON = 1e-06
MESH = pl.DeviceIdType.MESH


def exchange_kernel(
    n,
    part_ref,
    coef_ref,
    mask_ref,
    query_ref,
    row_ref,
    entry_ref,
    dec_ref,
    x_recv,
    coef_recv,
    q_recv,
    row_recv,
    f_recv,
    f_send,
    b_recv,
    b_send,
    e_send,
    e_recv,
    r_send,
    r_recv,
    xs_sem,
    xr_sem,
    cs_sem,
    cr_sem,
    qs_sem,
    qr_sem,
    ws_sem,
    wr_sem,
    fs_sem,
    fr_sem,
    bs_sem,
    br_sem,
    es_sem,
    er_sem,
    rs_sem,
    rr_sem,
):
    me = lax.axis_index("seq")
    side = lax.rem(me, PAIR)
    rank = me // PAIR
    ranks = n // PAIR
    partner = me + 1 - 2 * side
    heads = part_ref.shape[0]
    half = heads // PAIR
    slots = part_ref.shape[1]
    mine = side * half
    theirs = (1 - side) * half
    is_first = rank == 0
    is_last = rank == ranks - 1
    ahead = lax.rem(me + PAIR, n)
    behind = lax.rem(me + n - PAIR, n)

    def copy(src, dst, send, recv, to):
        return pltpu.make_async_remote_copy(
            src_ref=src,
            dst_ref=dst,
            send_sem=send,
            recv_sem=recv,
            device_id={"seq": to},
            device_id_type=MESH,
        )

    def x_copy(j, p):
        i = j * slots + p
        return copy(part_ref.at[theirs + j, p], x_recv.at[j, p], xs_sem.at[i], xr_sem.at[i], partner)

    def f_copy(j, p):
        i = j * slots + p
        return copy(f_send.at[j, p], f_recv.at[j, p], fs_sem.at[i], fr_sem.at[i], ahead)

    def b_copy(j, p):
        i = j * slots + p
        return copy(b_send.at[j, p], b_recv.at[j, p], bs_sem.at[i], br_sem.at[i], behind)

    def e_copy(j):
        return copy(e_send.at[j], e_recv.at[j], es_sem.at[j], er_sem.at[j], partner)

    def r_copy(j):
        return copy(r_send.at[j], r_recv.at[j], rs_sem.at[j], rr_sem.at[j], partner)

    coef_copy = copy(coef_ref.at[pl.ds(theirs, half)], coef_recv, cs_sem, cr_sem, partner)
    row_copy = copy(row_ref, row_recv, ws_sem, wr_sem, partner)
    q_copy = copy(query_ref.at[pl.ds(theirs, half)], q_recv, qs_sem, qr_sem, partner)

    barrier = pltpu.get_barrier_semaphore()
    pl.semaphore_signal(barrier, inc=1, device_id={"seq": partner}, device_id_type=MESH)

    @pl.when(jnp.logical_not(is_last))
    def _():
        pl.semaphore_signal(barrier, inc=1, device_id={"seq": ahead}, device_id_type=MESH)

    @pl.when(jnp.logical_not(is_first))
    def _():
        pl.semaphore_signal(barrier, inc=1, device_id={"seq": behind}, device_id_type=MESH)

    pl.semaphore_wait(barrier, 1 + jnp.where(is_first, 0, 1) + jnp.where(is_last, 0, 1))

    coef_copy.start()

    @pl.loop(0, half)
    def _(j):
        for p in range(slots):
            x_copy(j, p).start()

    row_copy.start()
    q_copy.start()

    @pl.when(is_first)
    def _():
        f_recv[...] = jnp.zeros_like(f_recv)

    @pl.when(is_last)
    def _():
        b_recv[...] = jnp.zeros_like(b_recv)

    coef_copy.wait()

    lag = jnp.where(is_last, 0, ranks - rank)
    low = side == 0

    def forward(j):
        acc_mine = None
        acc_theirs = None
        for p in range(slots):
            x_copy(j, p).wait_recv()

            @pl.when(jnp.logical_not(is_first))
            def _():
                f_copy(j, p).wait_recv()

            own = part_ref[mine + j, p]
            other = x_recv[j, p]
            c_own = coef_ref[mine + j, pl.ds(p, 1), :]
            c_other = coef_recv[j, pl.ds(p, 1), :]
            came = f_recv[j, p]
            middle = jnp.where(low, c_own, c_other) * came + jnp.where(low, own, other)
            after = jnp.where(low, c_other, c_own) * middle + jnp.where(low, other, own)
            f_send[j, p] = after

            @pl.when(jnp.logical_not(is_last))
            def _():
                f_copy(j, p).start()

            at_low = came * mask_ref[pl.ds(p, 1), :]
            at_high = middle * mask_ref[pl.ds(slots + p, 1), :]
            to_mine = jnp.where(low, at_low, at_high)
            to_theirs = jnp.where(low, at_high, at_low)
            acc_mine = to_mine if p == 0 else acc_mine + to_mine
            acc_theirs = to_theirs if p == 0 else acc_theirs + to_theirs
        entry_ref[mine + j] = acc_mine
        e_send[j] = acc_theirs
        e_copy(j).start()

    def backward(j):
        q_own = query_ref[mine + j].astype(jnp.bfloat16)
        q_other = q_recv[j].astype(jnp.bfloat16)
        total_own = None
        total_other = None
        for p in range(slots):

            @pl.when(jnp.logical_not(is_last))
            def _():
                b_copy(j, p).wait_recv()

            ended = mask_ref[pl.ds(2 * slots + p, 1), :]
            final = ended * f_send[j, p] + (1.0 - ended) * b_recv[j, p]
            b_send[j, p] = final

            @pl.when(jnp.logical_not(is_first))
            def _():
                b_copy(j, p).start()

            final_half = final.astype(jnp.bfloat16)
            got_own = jnp.dot(q_own, final_half, preferred_element_type=jnp.float32)
            got_other = jnp.dot(q_other, final_half, preferred_element_type=jnp.float32)
            got_own = jnp.where(row_ref[...] == float(p), got_own, 0.0)
            got_other = jnp.where(row_recv[...] == float(p), got_other, 0.0)
            total_own = got_own if p == 0 else total_own + got_own
            total_other = got_other if p == 0 else total_other + got_other
        dec_ref[mine + j] = total_own
        r_send[j] = total_other
        r_copy(j).start()

    row_copy.wait()
    q_copy.wait()

    @pl.loop(0, half + ranks)
    def _(t):
        @pl.when(t < half)
        def _():
            forward(t)

        @pl.when((t >= lag) & (t < half + lag))
        def _():
            backward(t - lag)

    @pl.loop(0, half)
    def _(j):
        e_copy(j).wait()
        entry_ref[theirs + j] = e_recv[j]
        r_copy(j).wait()
        dec_ref[theirs + j] = r_recv[j]
        for p in range(slots):
            x_copy(j, p).wait_send()

            @pl.when(jnp.logical_not(is_last))
            def _():
                f_copy(j, p).wait_send()

            @pl.when(jnp.logical_not(is_first))
            def _():
                b_copy(j, p).wait_send()


def exchange(n, parts, coef, masks, queries, rows):
    heads, slots = parts.shape[:2]
    half = heads // PAIR
    vectors = queries.shape[1]
    chunks = half * slots
    f32 = jnp.float32
    vmem = pl.BlockSpec(memory_space=pltpu.VMEM)
    dma = pltpu.SemaphoreType.DMA
    states = (half, slots, HDIM, HDIM)
    return pl.pallas_call(
        functools.partial(exchange_kernel, n),
        out_shape=(
            jax.ShapeDtypeStruct((heads, HDIM, HDIM), f32),
            jax.ShapeDtypeStruct((heads, vectors, HDIM), f32),
        ),
        in_specs=[vmem] * 5,
        out_specs=(vmem, vmem),
        scratch_shapes=[
            pltpu.VMEM(states, f32),
            pltpu.VMEM((half,) + coef.shape[1:], f32),
            pltpu.VMEM((half, vectors, HDIM), f32),
            pltpu.VMEM((vectors, HDIM), f32),
            pltpu.VMEM(states, f32),
            pltpu.VMEM(states, f32),
            pltpu.VMEM(states, f32),
            pltpu.VMEM(states, f32),
            pltpu.VMEM((half, HDIM, HDIM), f32),
            pltpu.VMEM((half, HDIM, HDIM), f32),
            pltpu.VMEM((half, vectors, HDIM), f32),
            pltpu.VMEM((half, vectors, HDIM), f32),
            dma((chunks,)),
            dma((chunks,)),
            dma,
            dma,
            dma,
            dma,
            dma,
            dma,
            dma((chunks,)),
            dma((chunks,)),
            dma((chunks,)),
            dma((chunks,)),
            dma((half,)),
            dma((half,)),
            dma((half,)),
            dma((half,)),
        ],
        compiler_params=pltpu.CompilerParams(
            collective_id=0, has_side_effects=True, vmem_limit_bytes=48 * 1024 * 1024
        ),
        name="exchange",
    )(parts, coef, masks, queries, rows)


def segment_ids(prompt_lengths, positions):
    boundary = jnp.cumsum(prompt_lengths)
    return jnp.sum((positions[:, None] >= boundary[None, :]).astype(jnp.int32), axis=1)


def local(
    n,
    query_in,
    key_in,
    value_in,
    log_decay,
    norm_gain,
    prompt_lengths,
    step_query,
    step_key,
    step_value,
    step_decay,
    row_prompt,
):
    f32 = jnp.float32
    tok = query_in.shape[0]
    heads = log_decay.shape[1]
    steps, rows = step_query.shape[:2]
    place = lax.axis_index("seq")
    first = place * tok
    pair_first = (place // PAIR) * (PAIR * tok)
    ends = jnp.cumsum(prompt_lengths)
    begins = ends - prompt_lengths
    segs = segment_ids(prompt_lengths, first + jnp.arange(tok, dtype=jnp.int32))
    slot = jnp.arange(PROMPTS, dtype=jnp.int32)

    def seg_before(token):
        return jnp.where(token > 0, segment_ids(prompt_lengths, (token - 1)[None])[0], -1)

    seg_front = seg_before(first)
    queries = query_in.reshape(tok, heads, HDIM)
    keys = key_in.reshape(tok, heads, HDIM)
    values = value_in.reshape(tok, heads, HDIM)
    cum = jnp.cumsum(log_decay, axis=0)

    last = jnp.clip(ends - first, 1, tok) - 1
    reached = jnp.sum(
        jnp.where((jnp.arange(tok)[None, :] == last[:, None])[:, :, None], cum[None], 0.0), axis=1
    )
    taken = (segs[None, :] == slot[:, None])[:, :, None]
    keep = jnp.where(taken, jnp.exp(jnp.where(taken, reached[:, None, :] - cum[None], 0.0)), 0.0)
    keyed = (keys.astype(f32)[None] * keep[..., None]).astype(jnp.bfloat16)
    parts = jnp.einsum("pshd,she->hpde", keyed, values, preferred_element_type=f32)
    coef = jnp.where(
        (ends <= first)[:, None], 1.0, jnp.where((begins < first)[:, None], jnp.exp(reached), 0.0)
    )
    coef = jnp.broadcast_to(coef.T[:, :, None], (heads, PROMPTS, HDIM))
    pair_last = pair_first + PAIR * tok
    marks = jnp.concatenate(
        [slot == seg_before(pair_first), slot == seg_before(pair_first + tok), ends <= pair_last]
    )
    marks = jnp.concatenate([marks, jnp.zeros((4,), bool)])
    masks = jnp.broadcast_to(marks.astype(f32)[:, None], (marks.shape[0], HDIM))

    step_q = step_query.reshape(steps, rows, heads, HDIM)
    vectors = jnp.transpose(step_q, (2, 0, 1, 3)).reshape(heads, steps * rows, HDIM).astype(f32)
    row_marks = jnp.broadcast_to(
        jnp.broadcast_to(row_prompt.astype(f32)[None, :], (steps, rows)).reshape(-1, 1),
        (steps * rows, HDIM),
    )
    entry, from_state = exchange(n, parts, coef, masks, vectors, row_marks)

    causal = jnp.arange(tok)[:, None] >= jnp.arange(tok)[None, :]
    linked = (causal & (segs[:, None] == segs[None, :]))[None]
    cum_heads = cum.T
    spread = cum_heads[:, :, None] - cum_heads[:, None, :]
    factor = jnp.where(linked, jnp.exp(jnp.where(linked, spread, 0.0)), 0.0)
    scores = jnp.einsum("thd,shd->hts", queries, keys, preferred_element_type=f32)
    weights = (scores * factor).astype(jnp.bfloat16)
    inner = jnp.einsum("hts,shd->thd", weights, values, preferred_element_type=f32)
    carried = jnp.exp(cum) * (segs == seg_front).astype(f32)[:, None]
    outer = (
        jnp.einsum("thd,hde->the", queries, entry.astype(jnp.bfloat16), preferred_element_type=f32)
        * carried[..., None]
    )
    mixed = (inner + outer).reshape(tok, heads * HDIM)

    step_k = step_key.reshape(steps, rows, heads, HDIM).astype(f32)
    step_v = step_value.reshape(steps, rows, heads, HDIM).astype(f32)
    step_qf = step_q.astype(f32)
    from_state = jnp.transpose(from_state.reshape(heads, steps, rows, HDIM), (1, 2, 0, 3))
    results = []
    for i in range(steps):
        decay = step_decay[i]
        total = jnp.sum(step_qf[i] * step_k[i], axis=-1)[..., None] * step_v[i]
        for j in range(i - 1, -1, -1):
            weight = jnp.exp(decay) * jnp.sum(step_qf[i] * step_k[j], axis=-1)
            total = total + weight[..., None] * step_v[j]
            decay = decay + step_decay[j]
        results.append(total + jnp.exp(decay)[..., None] * from_state[i])
    decoded = jnp.stack(results).reshape(steps, rows, heads * HDIM)

    squares, step_squares = lax.psum(
        (jnp.sum(mixed * mixed, axis=1), jnp.sum(decoded * decoded, axis=2)), "head"
    )
    scale = lax.rsqrt(squares / (HEAD_COUNT * HDIM) + EPSILON)
    attn_out = (mixed * scale[:, None] * norm_gain[None, :]).astype(jnp.bfloat16)
    step_scale = lax.rsqrt(step_squares / (HEAD_COUNT * HDIM) + EPSILON)
    decode_out = (decoded * step_scale[:, :, None] * norm_gain[None, None, :]).astype(jnp.bfloat16)
    return (attn_out, decode_out)


def solution(mesh):
    in_specs = (
        P("seq", "head"),
        P("seq", "head"),
        P("seq", "head"),
        P("seq", "head"),
        P("head"),
        P(),
        P(None, "seq", "head"),
        P(None, "seq", "head"),
        P(None, "seq", "head"),
        P(None, "seq", "head"),
        P("seq"),
    )
    out_specs = (P("seq", "head"), P(None, "seq", "head"))
    return jax.shard_map(
        functools.partial(local, mesh.shape["seq"]),
        mesh=mesh,
        in_specs=in_specs,
        out_specs=out_specs,
        check_vma=False,
    )
```

time: 467 us -> 197 us (0.42)
  waiting for transfers between devices: 235 us -> 0 us
  Pallas kernels: 0 us -> 141 us
  matrix products: 111 us -> 12 us
  local copies, waits for them, and re-layouts: 47 us -> 17.4 us
  blocking collectives: 29.1 us -> 5.67 us
  loops' own time: 13.2 us -> 0 us
  between operations: 15.6 us -> 3.04 us
    pallas_call x0 -> x1, Pallas kernels: none -> 141 us  [exchange(): pl.pallas_call(functools.partial(exchange_kernel, n), out_shape=(jax.Shap...]
    psum x1 -> x0, waiting for transfers between devices: 134 us -> none  [local(): prompt_state = lax.psum(candidates, 'seq')]
    all_gather x1 -> x0, waiting for transfers between devices: 102 us -> none  [carried_in(): gathered = jax.tree.map(lambda a: lax.all_gather(a, axis), part)]
    dot_general x11 -> x3, matrix products: 111 us -> 12 us  [the longest x1 4.74 us: local(): jnp.einsum('hts,shd->thd', weights, values, preferred_element_type=f32)]
    all_gather x1 -> x0, blocking collectives: 22.7 us -> none  [carried_in(): gathered = jax.tree.map(lambda a: lax.all_gather(a, axis), part)]
    another operation x2 -> x0, loops' own time: 13.2 us -> none  [the longest x1 13.2 us: local(): candidates = lax.map(prompt_end, jnp.arange(PROMPTS, dtype=jnp.int32))]
    gather x1 -> x0, local copies, waits for them, and re-layouts: 10.2 us -> none  [local(): row_states = jnp.take(prompt_state, row_prompt, axis=0)]
    another operation x14 -> x3, local copies, waits for them, and re-layouts: 6.97 us -> 0.74 us  [the longest x5 4.39 us: local(): decoded = jnp.stack(results)]
  transfers between devices with their start and end apart: 2 -> 0, of which waited for: 2 -> 0; matrix products, arithmetic and copies ran while one was open for 7% -> 0% of each run, Pallas kernels for 0% -> 0%
where the time goes in v1:
time: 197 us; the launch traced here: 196 us
  Pallas kernels  141 us (72%)
  local copies, waits for them, and re-layouts  17.4 us (9%)
  other arithmetic  16.4 us (8%)
  matrix products  12 us (6%)
  blocking collectives  5.67 us (3%)
  between operations  3.04 us (2%)
    pallas_call x1, Pallas kernels, exchange(): pl.pallas_call(functools.partial(exchange_kernel, n), out_shape=(jax.Shap...  141 us
    unnamed x49, local copies, waits for them, and re-layouts  8.14 us
    psum x1, blocking collectives, local(): lax.psum((jnp.sum(mixed * mixed, axis=1), jnp.sum(decoded * decoded, axis...  5.67 us
    dot_general x1, matrix products, local(): jnp.einsum('hts,shd->thd', weights, values, preferred_element_type=f32)  4.74 us
    dot_general x1, matrix products, local(): jnp.einsum('thd,hde->the', queries, entry.astype(jnp.bfloat16), preferred...  4.03 us

profile of v1, /device:TPU:0, one launch (start us, length us, event | category | flops | bytes accessed | tf_op | source)
XLA Modules:
  0.0 195.8 jit_solution(11478003734925083234)
XLA Ops:
  0.7 0.9 reduce-window.10
  5.0 1.5 copy.174
  6.4 1.6 bitcast_convert_fusion
  8.0 1.9 copy.122
  9.9 1.5 copy.175
  11.4 3.2 %fusion.part_ref = f32[16,4,128,128]{3,2,1,0:T(8,128)} fusion(f32[4,256,16]{1,0,2:T(4,128)S(1)} %exponential_select_fusion, f32[256,16,128]{0,2,1:T(8,128)S(1)} %copy.122, bf16[256,16,128,1]{2,1,0,3:T(8,128)(2,1)S(1)} %bitcast.261), kind=kOutput, calls=%fused_computation.1 | convolution fusion | flops 541065216 | bytes 7405568 | tf_op jit(solution)/shard_map/pshd,she->hpde/dot_general | solution.py:337
  16.2 0.9 fusion.47
  17.3 141.3 %exchange.1 = (f32[16,128,128]{2,1,0:T(8,128)S(1)}, f32[16,64,128]{2,1,0:T(8,128)S(1)}) custom-call(f32[16,4,128,128]{3,2,1,0:T(8,128)} %fusion.part_ref, f32[16,4,128]{2,1,0:T(4,128)S(1)} %broadcast_in_dim.97.coef_ref, f32[16,128]{1,0:T(8,128)S(1)} %broadcast_in_dim.98.mask_ref, f32[16,64,128]{2,1,0:T(8,128)S(1)} %bitcast.257, ...), custom_call_target="tpu_custom_call" | custom-call | tf_op jit(solution)/shard_map/exchange/pallas_call | solution.py:245
  158.7 4.7 %fusion.4 = f32[16,256,128]{1,2,0:T(8,128)} fusion(f32[16,256]{1,0:T(8,128)S(1)} %get-tuple-element.40, pred[256,256]{1,0:T(8,128)(4,1)S(1)} %fusion.19, bf16[256,2048]{1,0:T(8,128)(2,1)} %param.13, bf16[256,2048]{1,0:T(8,128)(2,1)} %param.12, bf16[256,2048]{1,0:T(8,128)(2,1)S(1)} %copy-done), kind=kOutput, calls=%fused_computation.9 | convolution fusion | flops 542113792 | bytes 5324800 | tf_op jit(solution)/shard_map/hts,shd->thd/dot_general | solution.py:364
  163.5 4.0 %multiply_reduce_fusion = (f32[256]{0:T(256)}, f32[256,16,128]{0,2,1:T(8,128)}) fusion(f32[256,16]{0,1:T(8,128)S(1)} %exponential_multiply_fusion, f32[16,128,128]{2,1,0:T(8,128)S(1)} %get-tuple-element.4, f32[16,256,128]{1,2,0:T(8,128)} %fusion.4, bf16[256,2048]{1,0:T(8,128)(2,1)S(1)} %copy-done), kind=kOutput, calls=%fused_computation.8 | convolution fusion | flops 136576768 | bytes 6308864 | tf_op jit(solution)/shard_map/thd,hde->the/dot_general | solution.py:367
  167.5 3.0 %copy.127 = f32[256,2048]{1,0:T(8,128)} copy(f32[256,2048]{0,1:T(8,128)} %bitcast.260) | data formatting | bytes 4194304 | tf_op jit(solution)/shard_map/reshape | solution.py:370
  171.7 0.8 fusion.34
  173.2 1.0 reduce_sum.166
  174.2 1.6 copy.185
  175.8 1.0 reduce_sum.168
  176.8 1.6 copy.181
  178.4 1.6 reduce_sum.164
  180.0 1.4 fusion.36
  181.4 0.8 copy.130
  182.6 0.8 copy.154
  183.4 0.8 copy.152
  186.5 5.7 %all-reduce = (f32[256]{0:T(256)S(1)}, f32[4,16]{1,0:T(4,128)S(1)}) all-reduce(f32[256]{0:T(256)S(1)} %copy-done.14, f32[4,16]{1,0:T(4,128)S(1)} %multiply_reduce_fusion.1), channel_id=1, replica_groups=mesh['seq'=8,'head'=4] {'head'}, use_global_device_ids=true, to_apply=%region_9.10 | all-reduce | flops 320 | bytes 2560 | tf_op jit(solution)/shard_map/psum | solution.py:387
  192.2 2.8 %multiply_convert_fusion.3 = bf16[256,2048]{1,0:T(8,128)(2,1)} fusion(f32[256,2048]{1,0:T(8,128)} %copy.127, f32[2048]{0:T(1024)S(1)} %copy-done.9, f32[256]{0:T(256)S(1)} %add_rsqrt_fusion.1), kind=kLoop, calls=%fused_computation.7 | loop fusion | flops 1572864 | bytes 3154944 | tf_op jit(solution)/shard_map/convert_element_type | solution.py:391
  195.0 0.8 multiply_convert_fusion.4
  (102 shorter events, 7.7 us)
Async XLA Ops:
  0.6 158.1 %copy-start = (bf16[256,2048]{1,0:T(8,128)(2,1)S(1)}, bf16[256,2048]{1,0:T(8,128)(2,1)}, u32[]{:S(2)}) copy-start(bf16[256,2048]{1,0:T(8,128)(2,1)} %param.11) | copy-start | bytes 3145732
  11.4 3.2 %copy-start.15 = (s32[4]{0:T(128)S(1)}, s32[4]{0:T(128)}, u32[]{:S(2)}) copy-start(s32[4]{0:T(128)} %param.16) | copy-start | bytes 52
  11.4 4.8 %copy-start.5 = (bf16[4,16,2048]{2,1,0:T(8,128)(2,1)S(1)}, bf16[4,16,2048]{2,1,0:T(8,128)(2,1)}, u32[]{:S(2)}) copy-start(bf16[4,16,2048]{2,1,0:T(8,128)(2,1)} %param.17) | copy-start | bytes 786436
  14.6 2.5 %copy-start.16 = (s32[16]{0:T(128)S(1)}, s32[16]{0:T(128)}, u32[]{:S(2)}) copy-start(s32[16]{0:T(128)} %param.21) | copy-start | bytes 196
  167.5 3.0 %copy-start.6 = (bf16[4,16,2048]{2,1,0:T(8,128)(2,1)S(1)}, bf16[4,16,2048]{2,1,0:T(8,128)(2,1)}, u32[]{:S(2)}) copy-start(bf16[4,16,2048]{2,1,0:T(8,128)(2,1)} %param.19) | copy-start | bytes 786436
  167.5 3.8 %copy-start.7 = (bf16[4,16,2048]{2,1,0:T(8,128)(2,1)S(1)}, bf16[4,16,2048]{2,1,0:T(8,128)(2,1)}, u32[]{:S(2)}) copy-start(bf16[4,16,2048]{2,1,0:T(8,128)(2,1)} %param.18) | copy-start | bytes 786436
  170.5 1.2 copy-start.1
  182.2 2.4 %copy-start.8 = (f32[4,16,16]{2,1,0:T(8,128)S(1)}, f32[4,16,16]{2,1,0:T(8,128)}, u32[]{:S(2)}) copy-start(f32[4,16,16]{2,1,0:T(8,128)} %param.20) | copy-start | bytes 12292
  182.2 2.5 %copy-start.13 = (f32[16,16]{1,0:T(8,128)S(1)}, f32[16,16]{1,0:T(8,128)}, u32[]{:S(2)}) copy-start(f32[16,16]{1,0:T(8,128)} %get-tuple-element.29) | copy-start | bytes 3076
  182.2 2.8 %copy-start.12 = (f32[16,16]{1,0:T(8,128)S(1)}, f32[16,16]{1,0:T(8,128)}, u32[]{:S(2)}) copy-start(f32[16,16]{1,0:T(8,128)} %get-tuple-element.31) | copy-start | bytes 3076
  182.2 2.9 %copy-start.11 = (f32[16,16]{1,0:T(8,128)S(1)}, f32[16,16]{1,0:T(8,128)}, u32[]{:S(2)}) copy-start(f32[16,16]{1,0:T(8,128)} %get-tuple-element.34) | copy-start | bytes 3076
  182.2 3.2 %copy-start.10 = (f32[16,16]{1,0:T(8,128)S(1)}, f32[16,16]{1,0:T(8,128)}, u32[]{:S(2)}) copy-start(f32[16,16]{1,0:T(8,128)} %get-tuple-element.33) | copy-start | bytes 3076
  182.2 3.6 %copy-start.2 = (f32[1,2,16,8,128]{4,3,2,1,0:T(8,128)S(1)}, f32[1,2,16,8,128]{4,3,2,1,0:T(8,128)}, u32[]{:S(2)}) copy-start(f32[1,2,16,8,128]{4,3,2,1,0:T(8,128)} %get-tuple-element.23) | copy-start | bytes 393220
  184.2 1.6 copy-start.3
  184.3 1.5 copy-start.4
  184.6 1.9 copy-start.14
  184.6 7.6 %copy-start.9 = (f32[2048]{0:T(1024)S(1)}, f32[2048]{0:T(1024)}, u32[]{:S(2)}) copy-start(f32[2048]{0:T(1024)} %param.15) | copy-start | bytes 24580

commit v2 on v1

v2 whole, which is shorter than its diff:
```python
import functools

import jax
import jax.numpy as jnp
from jax import lax
from jax.experimental import pallas as pl
from jax.experimental.pallas import tpu as pltpu
from jax.sharding import PartitionSpec as P

HEAD_COUNT = 64
HDIM = 128
BLOCK = 256
PROMPTS = 4
PAIR = 2


EPSILON = 1e-06
MESH = pl.DeviceIdType.MESH


def fused_kernel(
    n,
    steps,
    query_ref,
    key_ref,
    value_ref,
    cols_ref,
    cum_ref,
    bias_ref,
    coef_ref,
    mask_ref,
    sq_ref,
    sk_ref,
    sv_ref,
    weight_ref,
    row_ref,
    mixed_ref,
    square_ref,
    dec_ref,
    dsquare_ref,
    own_part,
    x_send,
    x_recv,
    coef_recv,
    q_send,
    q_recv,
    row_recv,
    f_recv,
    f_send,
    b_recv,
    b_send,
    e_send,
    e_recv,
    r_send,
    r_recv,
    xs_sem,
    xr_sem,
    cs_sem,
    cr_sem,
    qs_sem,
    qr_sem,
    ws_sem,
    wr_sem,
    fs_sem,
    fr_sem,
    bs_sem,
    br_sem,
    es_sem,
    er_sem,
    rs_sem,
    rr_sem,
):
    f32, bf16 = jnp.float32, jnp.bfloat16
    me = lax.axis_index("seq")
    side = lax.rem(me, PAIR)
    rank = me // PAIR
    ranks = n // PAIR
    partner = me + 1 - 2 * side
    half, slots = own_part.shape[:2]
    rows = sq_ref.shape[0] // steps
    mine = side * half
    theirs = (1 - side) * half
    is_first = rank == 0
    is_last = rank == ranks - 1
    low = side == 0
    ahead = lax.rem(me + PAIR, n)
    behind = lax.rem(me + n - PAIR, n)

    def copy(src, dst, send, recv, to):
        return pltpu.make_async_remote_copy(
            src_ref=src,
            dst_ref=dst,
            send_sem=send,
            recv_sem=recv,
            device_id={"seq": to},
            device_id_type=MESH,
        )

    def x_copy(j, p):
        i = j * slots + p
        return copy(x_send.at[j, p], x_recv.at[j, p], xs_sem.at[i], xr_sem.at[i], partner)

    def f_copy(j, p):
        i = j * slots + p
        return copy(f_send.at[j, p], f_recv.at[j, p], fs_sem.at[i], fr_sem.at[i], ahead)

    def b_copy(j, p):
        i = j * slots + p
        return copy(b_send.at[j, p], b_recv.at[j, p], bs_sem.at[i], br_sem.at[i], behind)

    def q_copy(j):
        return copy(q_send.at[j], q_recv.at[j], qs_sem.at[j], qr_sem.at[j], partner)

    def e_copy(j):
        return copy(e_send.at[j], e_recv.at[j], es_sem.at[j], er_sem.at[j], partner)

    def r_copy(j):
        return copy(r_send.at[j], r_recv.at[j], rs_sem.at[j], rr_sem.at[j], partner)

    coef_copy = copy(coef_ref.at[pl.ds(theirs, half)], coef_recv, cs_sem, cr_sem, partner)
    row_copy = copy(row_ref, row_recv, ws_sem, wr_sem, partner)

    def lanes(h):
        return pl.ds(pl.multiple_of(h * HDIM, HDIM), HDIM)

    barrier = pltpu.get_barrier_semaphore()
    pl.semaphore_signal(barrier, inc=1, device_id={"seq": partner}, device_id_type=MESH)

    @pl.when(jnp.logical_not(is_last))
    def _():
        pl.semaphore_signal(barrier, inc=1, device_id={"seq": ahead}, device_id_type=MESH)

    @pl.when(jnp.logical_not(is_first))
    def _():
        pl.semaphore_signal(barrier, inc=1, device_id={"seq": behind}, device_id_type=MESH)

    def make_parts(h, j, into):
        key = key_ref[:, lanes(h)].astype(f32)
        value = value_ref[:, lanes(h)]
        for p in range(slots):
            keyed = (key * cols_ref[h, :, p : p + 1]).astype(bf16)
            into[j, p] = lax.dot_general(
                keyed, value, (((0,), (0,)), ((), ())), preferred_element_type=f32
            )

    def within(h):
        query = query_ref[:, lanes(h)]
        scores = lax.dot_general(
            query, key_ref[:, lanes(h)], (((1,), (1,)), ((), ())), preferred_element_type=f32
        )
        spread = cols_ref[h, :, slots : slots + 1] - cum_ref[h] + bias_ref[...]
        weights = (scores * jnp.exp(spread)).astype(bf16)
        mixed_ref[:, lanes(h)] = jnp.dot(
            weights, value_ref[:, lanes(h)], preferred_element_type=f32
        )

    def across(h, entry):
        carried = cols_ref[h, :, slots + 1 : slots + 2]
        outer = jnp.dot(query_ref[:, lanes(h)], entry.astype(bf16), preferred_element_type=f32)
        mixed = mixed_ref[:, lanes(h)] + outer * carried
        mixed_ref[:, lanes(h)] = mixed
        square_ref[...] += mixed * mixed

    def own_steps(h):
        query = sq_ref[:, lanes(h)].astype(f32)
        key = sk_ref[:, lanes(h)].astype(f32)
        value = sv_ref[:, lanes(h)].astype(f32)
        weight = weight_ref[h]
        cut = lambda a, i: a[i * rows : (i + 1) * rows]
        spot = 0
        for i in range(steps):
            total = None
            for j in range(i + 1):
                dot = jnp.sum(cut(query, i) * cut(key, j), axis=1, keepdims=True)
                term = dot * weight[:, spot : spot + 1] * cut(value, j)
                total = term if j == 0 else total + term
                spot += 1
            dec_ref[i * rows : (i + 1) * rows, lanes(h)] = total

    def from_state(h, product):
        weight = weight_ref[h]
        spot = steps * (steps + 1) // 2
        for i in range(steps):
            at = slice(i * rows, (i + 1) * rows)
            out = dec_ref[at, lanes(h)] + weight[:, spot + i : spot + i + 1] * product[at]
            dec_ref[at, lanes(h)] = out
            dsquare_ref[at] += out * out

    square_ref[...] = jnp.zeros_like(square_ref)
    dsquare_ref[...] = jnp.zeros_like(dsquare_ref)
    make_parts(theirs, 0, x_send)
    pl.semaphore_wait(barrier, 1 + jnp.where(is_first, 0, 1) + jnp.where(is_last, 0, 1))
    coef_copy.start()

    @pl.loop(0, half)
    def _(j):
        @pl.when(j > 0)
        def _():
            make_parts(theirs + j, j, x_send)

        for p in range(slots):
            x_copy(j, p).start()

        @pl.when(j == 0)
        def _():
            row_copy.start()

        q_send[j] = sq_ref[:, lanes(theirs + j)].astype(f32)
        q_copy(j).start()
        make_parts(mine + j, j, own_part)

    @pl.when(is_first)
    def _():
        f_recv[...] = jnp.zeros_like(f_recv)

    @pl.when(is_last)
    def _():
        b_recv[...] = jnp.zeros_like(b_recv)

    coef_copy.wait()
    row_copy.wait()

    lag = jnp.where(is_last, 0, ranks - rank)

    def forward(j):
        acc_mine = None
        acc_theirs = None
        for p in range(slots):
            x_copy(j, p).wait_recv()

            @pl.when(jnp.logical_not(is_first))
            def _():
                f_copy(j, p).wait_recv()

            own = own_part[j, p]
            other = x_recv[j, p]
            c_own = coef_ref[mine + j, pl.ds(p, 1), :]
            c_other = coef_recv[j, pl.ds(p, 1), :]
            came = f_recv[j, p]
            middle = jnp.where(low, c_own, c_other) * came + jnp.where(low, own, other)
            after = jnp.where(low, c_other, c_own) * middle + jnp.where(low, other, own)
            f_send[j, p] = after

            @pl.when(jnp.logical_not(is_last))
            def _():
                f_copy(j, p).start()

            at_low = came * mask_ref[pl.ds(p, 1), :]
            at_high = middle * mask_ref[pl.ds(slots + p, 1), :]
            to_mine = jnp.where(low, at_low, at_high)
            to_theirs = jnp.where(low, at_high, at_low)
            acc_mine = to_mine if p == 0 else acc_mine + to_mine
            acc_theirs = to_theirs if p == 0 else acc_theirs + to_theirs
        e_send[j] = acc_theirs
        e_copy(j).start()
        within(mine + j)
        across(mine + j, acc_mine)

    def backward(j):
        q_copy(j).wait_recv()
        q_own = sq_ref[:, lanes(mine + j)]
        q_other = q_recv[j].astype(bf16)
        total_own = None
        total_other = None
        for p in range(slots):

            @pl.when(jnp.logical_not(is_last))
            def _():
                b_copy(j, p).wait_recv()

            ended = mask_ref[pl.ds(2 * slots + p, 1), :]
            final = ended * f_send[j, p] + (1.0 - ended) * b_recv[j, p]
            b_send[j, p] = final

            @pl.when(jnp.logical_not(is_first))
            def _():
                b_copy(j, p).start()

            final_half = final.astype(bf16)
            got_own = jnp.dot(q_own, final_half, preferred_element_type=f32)
            got_other = jnp.dot(q_other, final_half, preferred_element_type=f32)
            got_own = jnp.where(row_ref[...] == float(p), got_own, 0.0)
            got_other = jnp.where(row_recv[...] == float(p), got_other, 0.0)
            total_own = got_own if p == 0 else total_own + got_own
            total_other = got_other if p == 0 else total_other + got_other
        r_send[j] = total_other
        r_copy(j).start()
        from_state(mine + j, total_own)

    @pl.loop(0, half + ranks)
    def _(t):
        @pl.when(t < half)
        def _():
            own_steps(t)
            own_steps(half + t)
            forward(t)

        @pl.when((t >= lag) & (t < half + lag))
        def _():
            backward(t - lag)

        @pl.when(t < half)
        def _():
            within(theirs + t)

    @pl.loop(0, half)
    def _(j):
        e_copy(j).wait()
        across(theirs + j, e_recv[j])

    @pl.loop(0, half)
    def _(j):
        r_copy(j).wait()
        from_state(theirs + j, r_recv[j])
        q_copy(j).wait_send()
        for p in range(slots):
            x_copy(j, p).wait_send()

            @pl.when(jnp.logical_not(is_last))
            def _():
                f_copy(j, p).wait_send()

            @pl.when(jnp.logical_not(is_first))
            def _():
                b_copy(j, p).wait_send()


def fused(n, steps, *operands):
    query, coef, step = operands[0], operands[6], operands[8]
    tok, width = query.shape
    heads, slots = coef.shape[:2]
    half = heads // PAIR
    vectors = step.shape[0]
    chunks = half * slots
    f32 = jnp.float32
    vmem = pl.BlockSpec(memory_space=pltpu.VMEM)
    dma = pltpu.SemaphoreType.DMA
    states = pltpu.VMEM((half, slots, HDIM, HDIM), f32)
    entries = pltpu.VMEM((half, HDIM, HDIM), f32)
    products = pltpu.VMEM((half, vectors, HDIM), f32)
    return pl.pallas_call(
        functools.partial(fused_kernel, n, steps),
        out_shape=(
            jax.ShapeDtypeStruct((tok, width), f32),
            jax.ShapeDtypeStruct((tok, HDIM), f32),
            jax.ShapeDtypeStruct((vectors, width), f32),
            jax.ShapeDtypeStruct((vectors, HDIM), f32),
        ),
        in_specs=[vmem] * len(operands),
        out_specs=(vmem,) * 4,
        scratch_shapes=[
            states,
            states,
            states,
            pltpu.VMEM((half,) + coef.shape[1:], f32),
            products,
            products,
            pltpu.VMEM((vectors, HDIM), f32),
            states,
            states,
            states,
            states,
            entries,
            entries,
            products,
            products,
            dma((chunks,)),
            dma((chunks,)),
            dma,
            dma,
            dma((half,)),
            dma((half,)),
            dma,
            dma,
            dma((chunks,)),
            dma((chunks,)),
            dma((chunks,)),
            dma((chunks,)),
            dma((half,)),
            dma((half,)),
            dma((half,)),
            dma((half,)),
        ],
        compiler_params=pltpu.CompilerParams(
            collective_id=0, has_side_effects=True, vmem_limit_bytes=56 * 1024 * 1024
        ),
        name="fused",
    )(*operands)


def segment_ids(prompt_lengths, positions):
    boundary = jnp.cumsum(prompt_lengths)
    return jnp.sum((positions[:, None] >= boundary[None, :]).astype(jnp.int32), axis=1)


def local(
    n,
    query_in,
    key_in,
    value_in,
    log_decay,
    norm_gain,
    prompt_lengths,
    step_query,
    step_key,
    step_value,
    step_decay,
    row_prompt,
):
    f32 = jnp.float32
    tok = query_in.shape[0]
    heads = log_decay.shape[1]
    steps, rows = step_query.shape[:2]
    place = lax.axis_index("seq")
    first = place * tok
    pair_first = (place // PAIR) * (PAIR * tok)
    ends = jnp.cumsum(prompt_lengths)
    begins = ends - prompt_lengths
    segs = segment_ids(prompt_lengths, first + jnp.arange(tok, dtype=jnp.int32))
    slot = jnp.arange(PROMPTS, dtype=jnp.int32)

    def seg_before(token):
        return jnp.where(token > 0, segment_ids(prompt_lengths, (token - 1)[None])[0], -1)

    seg_front = seg_before(first)
    cum = jnp.cumsum(log_decay, axis=0)

    last = jnp.clip(ends - first, 1, tok) - 1
    reached = jnp.sum(
        jnp.where((jnp.arange(tok)[None, :] == last[:, None])[:, :, None], cum[None], 0.0), axis=1
    )
    taken = (segs[None, :] == slot[:, None])[:, :, None]
    keep = jnp.where(taken, jnp.exp(jnp.where(taken, reached[:, None, :] - cum[None], 0.0)), 0.0)
    carried = jnp.exp(cum) * (segs == seg_front).astype(f32)[:, None]
    cols = jnp.transpose(jnp.concatenate([keep, cum[None], carried[None]]), (2, 1, 0))
    cum_rows = cum.T[:, None, :]
    causal = jnp.arange(tok)[:, None] >= jnp.arange(tok)[None, :]
    linked = causal & (segs[:, None] == segs[None, :])
    bias = jnp.where(linked, 0.0, -jnp.inf)
    coef = jnp.where(
        (ends <= first)[:, None], 1.0, jnp.where((begins < first)[:, None], jnp.exp(reached), 0.0)
    )
    coef = jnp.broadcast_to(coef.T[:, :, None], (heads, PROMPTS, HDIM))
    pair_last = pair_first + PAIR * tok
    marks = jnp.concatenate(
        [slot == seg_before(pair_first), slot == seg_before(pair_first + tok), ends <= pair_last]
    )
    marks = jnp.concatenate([marks, jnp.zeros((4,), bool)])
    masks = jnp.broadcast_to(marks.astype(f32)[:, None], (marks.shape[0], HDIM))

    shares, wholes = [], []
    for i in range(steps):
        for j in range(i + 1):
            shares.append(jnp.exp(jnp.sum(step_decay[j + 1 : i + 1], axis=0)))
        wholes.append(jnp.exp(jnp.sum(step_decay[: i + 1], axis=0)))
    step_weights = jnp.transpose(jnp.stack(shares + wholes), (2, 1, 0))
    row_marks = jnp.broadcast_to(
        jnp.broadcast_to(row_prompt.astype(f32)[None, :], (steps, rows)).reshape(-1, 1),
        (steps * rows, HDIM),
    )
    flat = lambda a: a.reshape(steps * rows, -1)
    mixed, mixed_sq, decoded, decoded_sq = fused(
        n,
        steps,
        query_in,
        key_in,
        value_in,
        cols,
        cum_rows,
        bias,
        coef,
        masks,
        flat(step_query),
        flat(step_key),
        flat(step_value),
        step_weights,
        row_marks,
    )
    squares, step_squares = lax.psum(
        (jnp.sum(mixed_sq, axis=1), jnp.sum(decoded_sq, axis=1)), "head"
    )
    scale = lax.rsqrt(squares / (HEAD_COUNT * HDIM) + EPSILON)
    attn_out = (mixed * scale[:, None] * norm_gain[None, :]).astype(jnp.bfloat16)
    step_scale = lax.rsqrt(step_squares / (HEAD_COUNT * HDIM) + EPSILON)
    decode_out = (decoded * step_scale[:, None] * norm_gain[None, :]).astype(jnp.bfloat16)
    return (attn_out, decode_out.reshape(step_query.shape))


def solution(mesh):
    in_specs = (
        P("seq", "head"),
        P("seq", "head"),
        P("seq", "head"),
        P("seq", "head"),
        P("head"),
        P(),
        P(None, "seq", "head"),
        P(None, "seq", "head"),
        P(None, "seq", "head"),
        P(None, "seq", "head"),
        P("seq"),
    )
    out_specs = (P("seq", "head"), P(None, "seq", "head"))
    return jax.shard_map(
        functools.partial(local, mesh.shape["seq"]),
        mesh=mesh,
        in_specs=in_specs,
        out_specs=out_specs,
        check_vma=False,
    )
```

time: 197 us -> 134 us (0.68)
  Pallas kernels: 141 us -> 103 us
  matrix products: 12 us -> 0 us
  local copies, waits for them, and re-layouts: 17.4 us -> 8.76 us
  other arithmetic: 16.4 us -> 13.1 us
    pallas_call x1, Pallas kernels: 141 us -> 103 us  [fused(): pl.pallas_call(functools.partial(fused_kernel, n, steps), out_shape=(jax....]
    dot_general x3 -> x0, matrix products: 12 us -> none  [the longest x1 4.74 us: local(): jnp.einsum('hts,shd->thd', weights, values, preferred_element_type=f32)]
    unnamed x49 -> x6, local copies, waits for them, and re-layouts: 8.14 us -> 0.02 us
    reshape x1 -> x0, local copies, waits for them, and re-layouts: 3 us -> none  [local(): mixed = (inner + outer).reshape(tok, heads * HDIM)]
    convert_element_type x5 -> x1, other arithmetic: 3.34 us -> 0.82 us  [local(): (decoded * step_scale[:, None] * norm_gain[None, :]).astype(jnp.bfloat16)]
    concatenate x0 -> x1, local copies, waits for them, and re-layouts: none -> 2.02 us  [local(): jnp.concatenate([keep, cum[None], carried[None]])]
    convert_element_type x2 -> x0, local copies, waits for them, and re-layouts: 1.97 us -> none  [the longest x1 1.93 us: local(): keyed = (keys.astype(f32)[None] * keep[..., None]).astype(jnp.bfloat16)]
    reduce_sum x11 -> x5, other arithmetic: 4.47 us -> 4.35 us  [the longest x3 2.4 us: local(): wholes.append(jnp.exp(jnp.sum(step_decay[:i + 1], axis=0)))]
where the time goes in v2:
time: 134 us; the launch traced here: 133 us
  Pallas kernels  103 us (77%)
  other arithmetic  13.1 us (10%)
  local copies, waits for them, and re-layouts  8.76 us (7%)
  blocking collectives  5.67 us (4%)
  between operations  2.79 us (2%)
    pallas_call x1, Pallas kernels, fused(): pl.pallas_call(functools.partial(fused_kernel, n, steps), out_shape=(jax....  103 us
    psum x1, blocking collectives, local(): lax.psum((jnp.sum(mixed_sq, axis=1), jnp.sum(decoded_sq, axis=1)), 'head')  5.67 us
    convert_element_type x1, other arithmetic, local(): (mixed * scale[:, None] * norm_gain[None, :]).astype(jnp.bfloat16)  2.8 us

profile of v2, /device:TPU:0, one launch (start us, length us, event | category | flops | bytes accessed | tf_op | source)
XLA Modules:
  0.0 133.4 jit_solution(14112389178646799400)
XLA Ops:
  0.7 0.8 reduce-window.10
  1.5 0.7 fusion.3
  4.3 0.7 convert_element_type.68
  5.1 0.7 broadcast_compare_fusion
  5.9 0.7 broadcast_in_dim.136.mask_ref
  6.6 0.8 reduce_sum.143
  7.4 0.6 reduce-window.11
  8.4 0.6 copy.95
  9.3 0.8 slice_reduce_fusion
  10.2 0.7 broadcast_in_dim.135.coef_ref
  10.8 0.8 slice_reduce_fusion.3
  11.7 0.7 broadcast_in_dim.139.row_ref
  12.3 0.8 slice_exponential_fusion
  13.6 0.2 copy.106
  14.5 0.2 copy.99
  15.0 1.2 stack.2
  16.2 0.8 fusion.1.bias_ref
  17.0 2.0 %copy.96 = f32[6,256,16]{0,1,2:T(8,128)} copy(f32[6,256,16]{1,2,0:T(8,128)S(1)} %pad_maximum_fusion) | data formatting | bytes 196608 | tf_op jit(solution)/shard_map/concatenate | solution.py:435
  19.0 103.1 %fused.1 = (f32[256,2048]{1,0:T(8,128)}, f32[256,128]{1,0:T(8,128)}, f32[64,2048]{1,0:T(8,128)}, f32[64,128]{1,0:T(8,128)}) custom-call(bf16[256,2048]{1,0:T(8,128)(2,1)} %query_ref.1, bf16[256,2048]{1,0:T(8,128)(2,1)} %key_ref.1, bf16[256,2048]{1,0:T(8,128)(2,1)} %value_ref.1, f32[16,256,6]{2,1,0:T(8,128)} %bitcast.51, f32[16,1,256]{2,1,0:T(1,128)} %bitcast.57, ...), custom_call_target="tpu_custom_call" | custom-call | tf_op jit(solution)/shard_map/fused/pallas_call | solution.py:341
  122.2 0.9 reduce_sum.145
  123.1 1.0 reduce_sum.144
  124.1 5.7 %all-reduce = (f32[256]{0:T(256)S(1)}, f32[64]{0:T(128)S(1)}) all-reduce(f32[256]{0:T(256)S(1)} %reduce_sum.144, f32[64]{0:T(128)S(1)} %reduce_sum.145), channel_id=1, replica_groups=mesh['seq'=8,'head'=4] {'head'}, use_global_device_ids=true, to_apply=%region_15.16 | all-reduce | flops 320 | bytes 2560 | tf_op jit(solution)/shard_map/psum | solution.py:479
  129.8 2.8 %multiply_convert_fusion = bf16[256,2048]{1,0:T(8,128)(2,1)} fusion(f32[256,2048]{1,0:T(8,128)} %get-tuple-element.6, f32[2048]{0:T(1024)S(1)} %copy-done.2, f32[256]{0:T(256)S(1)} %add_rsqrt_fusion), kind=kLoop, calls=%fused_computation | loop fusion | flops 1572864 | bytes 3154944 | tf_op jit(solution)/shard_map/convert_element_type | solution.py:483
  132.6 0.8 multiply_convert_fusion.1
  (44 shorter events, 2.6 us)
Async XLA Ops:
  0.6 6.8 %copy-start = (f32[256,16]{0,1:T(8,128)S(1)}, f32[256,16]{0,1:T(8,128)}, u32[]{:S(2)}) copy-start(f32[256,16]{0,1:T(8,128)} %param.14) | copy-start | bytes 49156
  19.0 110.8 %copy-start.2 = (f32[2048]{0:T(1024)S(1)}, f32[2048]{0:T(1024)}, u32[]{:S(2)}) copy-start(f32[2048]{0:T(1024)} %param.15) | copy-start | bytes 24580
  122.2 10.4 %copy-start.1 = (f32[64,2048]{1,0:T(8,128)S(1)}, f32[64,2048]{1,0:T(8,128)}, u32[]{:S(2)}) copy-start(f32[64,2048]{1,0:T(8,128)} %get-tuple-element.8) | copy-start | bytes 1572868

commit v3 on v2

--- a/solution.py
+++ b/solution.py
@@ -49,6 +49,12 @@
     f_send,
     b_recv,
     b_send,
+    pair_part,
+    t_recv,
+    t_send,
+    e_mine,
+    acc_sq,
+    acc_dsq,
     e_send,
     e_recv,
     r_send,
@@ -65,6 +71,8 @@
     fr_sem,
     bs_sem,
     br_sem,
+    ts_sem,
+    tr_sem,
     es_sem,
     er_sem,
     rs_sem,
@@ -120,6 +128,8 @@
     coef_copy = copy(coef_ref.at[pl.ds(theirs, half)], coef_recv, cs_sem, cr_sem, partner)
     row_copy = copy(row_ref, row_recv, ws_sem, wr_sem, partner)
 
+    t_copy = copy(t_send, t_recv, ts_sem, tr_sem, behind)
+
     def lanes(h):
         return pl.ds(pl.multiple_of(h * HDIM, HDIM), HDIM)
 
@@ -159,7 +169,7 @@
         outer = jnp.dot(query_ref[:, lanes(h)], entry.astype(bf16), preferred_element_type=f32)
         mixed = mixed_ref[:, lanes(h)] + outer * carried
         mixed_ref[:, lanes(h)] = mixed
-        square_ref[...] += mixed * mixed
+        acc_sq[...] += mixed * mixed
 
     def own_steps(h):
         query = sq_ref[:, lanes(h)].astype(f32)
@@ -184,10 +194,10 @@
             at = slice(i * rows, (i + 1) * rows)
             out = dec_ref[at, lanes(h)] + weight[:, spot + i : spot + i + 1] * product[at]
             dec_ref[at, lanes(h)] = out
-            dsquare_ref[at] += out * out
-
-    square_ref[...] = jnp.zeros_like(square_ref)
-    dsquare_ref[...] = jnp.zeros_like(dsquare_ref)
+            acc_dsq[at] += out * out
+
+    acc_sq[...] = jnp.zeros_like(acc_sq)
+    acc_dsq[...] = jnp.zeros_like(acc_dsq)
     make_parts(theirs, 0, x_send)
     pl.semaphore_wait(barrier, 1 + jnp.where(is_first, 0, 1) + jnp.where(is_last, 0, 1))
     coef_copy.start()
@@ -220,31 +230,68 @@
     coef_copy.wait()
     row_copy.wait()
 
-    lag = jnp.where(is_last, 0, ranks - rank)
+    @pl.when(is_last)
+    def _():
+        t_recv[...] = jnp.ones_like(t_recv)
+
+    lag_f = rank
+    lag_b = ranks - 1 - rank
+    lag_d = jnp.maximum(lag_f, lag_b)
+
+    def relay_decay():
+        @pl.when(jnp.logical_not(is_last))
+        def _():
+            t_copy.wait_recv()
+
+        @pl.when(jnp.logical_not(is_first))
+        def _():
+            t_send[...] = t_recv[...] * coef_recv[...] * coef_ref[pl.ds(mine, half)]
+            t_copy.start()
+
+    def rows_of(j, p):
+        c_own = coef_ref[mine + j, pl.ds(p, 1), :]
+        c_other = coef_recv[j, pl.ds(p, 1), :]
+        return jnp.where(low, c_own, c_other), jnp.where(low, c_other, c_own)
+
+    def combine(j):
+        for p in range(slots):
+            x_copy(j, p).wait_recv()
+            own = own_part[j, p]
+            other = x_recv[j, p]
+            c_low, c_high = rows_of(j, p)
+            pair = c_high * jnp.where(low, own, other) + jnp.where(low, other, own)
+            pair_part[j, p] = pair
+
+            @pl.when(is_first)
+            def _():
+                f_send[j, p] = pair
+
+                @pl.when(jnp.logical_not(is_last))
+                def _():
+                    f_copy(j, p).start()
+
+            @pl.when(is_last & jnp.logical_not(is_first))
+            def _():
+                b_send[j, p] = pair
+                b_copy(j, p).start()
 
     def forward(j):
         acc_mine = None
         acc_theirs = None
         for p in range(slots):
-            x_copy(j, p).wait_recv()
+            c_low, c_high = rows_of(j, p)
 
             @pl.when(jnp.logical_not(is_first))
             def _():
                 f_copy(j, p).wait_recv()
-
-            own = own_part[j, p]
-            other = x_recv[j, p]
-            c_own = coef_ref[mine + j, pl.ds(p, 1), :]
-            c_other = coef_recv[j, pl.ds(p, 1), :]
+                f_send[j, p] = (c_low * c_high) * f_recv[j, p] + pair_part[j, p]
+
+                @pl.when(jnp.logical_not(is_last))
+                def _():
+                    f_copy(j, p).start()
+
             came = f_recv[j, p]
-            middle = jnp.where(low, c_own, c_other) * came + jnp.where(low, own, other)
-            after = jnp.where(low, c_other, c_own) * middle + jnp.where(low, other, own)
-            f_send[j, p] = after
-
-            @pl.when(jnp.logical_not(is_last))
-            def _():
-                f_copy(j, p).start()
-
+            middle = c_low * came + jnp.where(low, own_part[j, p], x_recv[j, p])
             at_low = came * mask_ref[pl.ds(p, 1), :]
             at_high = middle * mask_ref[pl.ds(slots + p, 1), :]
             to_mine = jnp.where(low, at_low, at_high)
@@ -253,29 +300,28 @@
             acc_theirs = to_theirs if p == 0 else acc_theirs + to_theirs
         e_send[j] = acc_theirs
         e_copy(j).start()
-        within(mine + j)
-        across(mine + j, acc_mine)
+        e_mine[j] = acc_mine
 
     def backward(j):
+        for p in range(slots):
+
+            @pl.when(jnp.logical_not(is_last))
+            def _():
+                b_copy(j, p).wait_recv()
+
+                @pl.when(jnp.logical_not(is_first))
+                def _():
+                    b_send[j, p] = b_recv[j, p] + t_recv[j, pl.ds(p, 1), :] * pair_part[j, p]
+                    b_copy(j, p).start()
+
+    def decode(j):
         q_copy(j).wait_recv()
         q_own = sq_ref[:, lanes(mine + j)]
         q_other = q_recv[j].astype(bf16)
         total_own = None
         total_other = None
         for p in range(slots):
-
-            @pl.when(jnp.logical_not(is_last))
-            def _():
-                b_copy(j, p).wait_recv()
-
-            ended = mask_ref[pl.ds(2 * slots + p, 1), :]
-            final = ended * f_send[j, p] + (1.0 - ended) * b_recv[j, p]
-            b_send[j, p] = final
-
-            @pl.when(jnp.logical_not(is_first))
-            def _():
-                b_copy(j, p).start()
-
+            final = t_recv[j, pl.ds(p, 1), :] * f_send[j, p] + b_recv[j, p]
             final_half = final.astype(bf16)
             got_own = jnp.dot(q_own, final_half, preferred_element_type=f32)
             got_other = jnp.dot(q_other, final_half, preferred_element_type=f32)
@@ -287,21 +333,38 @@
         r_copy(j).start()
         from_state(mine + j, total_own)
 
-    @pl.loop(0, half + ranks)
+    @pl.loop(0, half + ranks - 1)
     def _(t):
         @pl.when(t < half)
         def _():
             own_steps(t)
             own_steps(half + t)
-            forward(t)
-
-        @pl.when((t >= lag) & (t < half + lag))
-        def _():
-            backward(t - lag)
+            within(mine + t)
+            within(theirs + t)
+
+        @pl.when(t == lag_b)
+        def _():
+            relay_decay()
 
         @pl.when(t < half)
         def _():
-            within(theirs + t)
+            combine(t)
+
+        @pl.when((t >= lag_f) & (t < half + lag_f))
+        def _():
+            forward(t - lag_f)
+
+        @pl.when((t >= lag_b) & (t < half + lag_b))
+        def _():
+            backward(t - lag_b)
+
+        @pl.when((t >= lag_d) & (t < half + lag_d))
+        def _():
+            decode(t - lag_d)
+
+        @pl.when((t >= lag_f) & (t < half + lag_f))
+        def _():
+            across(mine + t - lag_f, e_mine[t - lag_f])
 
     @pl.loop(0, half)
     def _(j):
@@ -323,6 +386,13 @@
             @pl.when(jnp.logical_not(is_first))
             def _():
                 b_copy(j, p).wait_send()
+
+    @pl.when(jnp.logical_not(is_first))
+    def _():
+        t_copy.wait_send()
+
+    square_ref[...] = jnp.sum(acc_sq[...], axis=1, keepdims=True)
+    dsquare_ref[...] = jnp.sum(acc_dsq[...], axis=1, keepdims=True)
 
 
 def fused(n, steps, *operands):
@@ -336,15 +406,16 @@
     vmem = pl.BlockSpec(memory_space=pltpu.VMEM)
     dma = pltpu.SemaphoreType.DMA
     states = pltpu.VMEM((half, slots, HDIM, HDIM), f32)
+    decays = pltpu.VMEM((half,) + coef.shape[1:], f32)
     entries = pltpu.VMEM((half, HDIM, HDIM), f32)
     products = pltpu.VMEM((half, vectors, HDIM), f32)
     return pl.pallas_call(
         functools.partial(fused_kernel, n, steps),
         out_shape=(
             jax.ShapeDtypeStruct((tok, width), f32),
-            jax.ShapeDtypeStruct((tok, HDIM), f32),
+            jax.ShapeDtypeStruct((tok, 1), f32),
             jax.ShapeDtypeStruct((vectors, width), f32),
-            jax.ShapeDtypeStruct((vectors, HDIM), f32),
+            jax.ShapeDtypeStruct((vectors, 1), f32),
         ),
         in_specs=[vmem] * len(operands),
         out_specs=(vmem,) * 4,
@@ -352,7 +423,7 @@
             states,
             states,
             states,
-            pltpu.VMEM((half,) + coef.shape[1:], f32),
+            decays,
             products,
             products,
             pltpu.VMEM((vectors, HDIM), f32),
@@ -360,6 +431,12 @@
             states,
             states,
             states,
+            states,
+            decays,
+            decays,
+            entries,
+            pltpu.VMEM((tok, HDIM), f32),
+            pltpu.VMEM((vectors, HDIM), f32),
             entries,
             entries,
             products,
@@ -376,6 +453,8 @@
             dma((chunks,)),
             dma((chunks,)),
             dma((chunks,)),
+            dma,
+            dma,
             dma((half,)),
             dma((half,)),
             dma((half,)),
@@ -448,12 +527,15 @@
     marks = jnp.concatenate([marks, jnp.zeros((4,), bool)])
     masks = jnp.broadcast_to(marks.astype(f32)[:, None], (marks.shape[0], HDIM))
 
-    shares, wholes = [], []
-    for i in range(steps):
-        for j in range(i + 1):
-            shares.append(jnp.exp(jnp.sum(step_decay[j + 1 : i + 1], axis=0)))
-        wholes.append(jnp.exp(jnp.sum(step_decay[: i + 1], axis=0)))
-    step_weights = jnp.transpose(jnp.stack(shares + wholes), (2, 1, 0))
+    shares = [
+        [float(j < k <= i) for k in range(steps)] for i in range(steps) for j in range(i + 1)
+    ]
+    wholes = [[float(k <= i) for k in range(steps)] for i in range(steps)]
+    step_weights = jnp.exp(
+        jnp.einsum(
+            "irh,wi->hrw", step_decay, jnp.array(shares + wholes, f32), precision=lax.Precision.HIGHEST
+        )
+    )
     row_marks = jnp.broadcast_to(
         jnp.broadcast_to(row_prompt.astype(f32)[None, :], (steps, rows)).reshape(-1, 1),
         (steps * rows, HDIM),
@@ -477,7 +559,7 @@
         row_marks,
     )
     squares, step_squares = lax.psum(
-        (jnp.sum(mixed_sq, axis=1), jnp.sum(decoded_sq, axis=1)), "head"
+        (mixed_sq[:, 0], decoded_sq[:, 0]), "head"
     )
     scale = lax.rsqrt(squares / (HEAD_COUNT * HDIM) + EPSILON)
     attn_out = (mixed * scale[:, None] * norm_gain[None, :]).astype(jnp.bfloat16)

time: 134 us -> 111 us (0.83)
  Pallas kernels: 103 us -> 83.7 us
  other arithmetic: 13.1 us -> 10.6 us
  local copies, waits for them, and re-layouts: 8.76 us -> 6.64 us
    pallas_call x1, Pallas kernels: 103 us -> 83.7 us  [fused(): pl.pallas_call(functools.partial(fused_kernel, n, steps), out_shape=(jax....]
    reduce_sum x5 -> x0, other arithmetic: 4.35 us -> none  [the longest x3 2.4 us: local(): wholes.append(jnp.exp(jnp.sum(step_decay[:i + 1], axis=0)))]
    pallas_call x0 -> x2, other arithmetic: none -> 1.94 us  [fused(): pl.pallas_call(functools.partial(fused_kernel, n, steps), out_shape=(jax....]
    exp x15 -> x2, local copies, waits for them, and re-layouts: 2.55 us -> 0.88 us  [local(): jnp.exp(jnp.einsum('irh,wi->hrw', step_decay, jnp.array(shares + wholes,...]
where the time goes in v3:
time: 111 us; the launch traced here: 110 us
  Pallas kernels  83.7 us (75%)
  other arithmetic  10.6 us (10%)
  local copies, waits for them, and re-layouts  6.64 us (6%)
  blocking collectives  5.67 us (5%)
  between operations  2.74 us (2%)
    pallas_call x1, Pallas kernels, fused(): pl.pallas_call(functools.partial(fused_kernel, n, steps), out_shape=(jax....  83.7 us
    psum x1, blocking collectives, local(): squares, step_squares = lax.psum((mixed_sq[:, 0], decoded_sq[:, 0]), 'head')  5.67 us
    convert_element_type x1, other arithmetic, local(): (mixed * scale[:, None] * norm_gain[None, :]).astype(jnp.bfloat16)  2.8 us

profile of v3, /device:TPU:0, one launch (start us, length us, event | category | flops | bytes accessed | tf_op | source)
XLA Modules:
  0.0 110.4 jit_solution(11229207372575305729)
XLA Ops:
  0.7 0.8 reduce-window.10
  1.5 0.7 fusion.5
  4.3 0.7 convert_element_type.68
  5.0 0.1 convert_reduce_fusion
  5.1 0.7 broadcast_compare_fusion
  5.9 0.7 broadcast_in_dim.136.mask_ref
  6.6 0.7 copy_bitcast_fusion
  7.3 0.6 reduce-window.11
  7.9 0.2 slice_reduce_fusion
  8.3 0.6 copy.61
  8.9 0.1 select_reduce_fusion
  9.1 0.1 copy.64
  9.2 0.7 broadcast_in_dim.135.coef_ref
  9.9 0.7 broadcast_in_dim.139.row_ref
  10.7 1.0 fusion.2
  11.8 0.8 copy.67
  12.6 0.8 fusion.1.bias_ref
  13.4 2.0 %copy.62 = f32[6,256,16]{0,1,2:T(8,128)} copy(f32[6,256,16]{1,2,0:T(8,128)S(1)} %pad_maximum_fusion) | data formatting | bytes 196608 | tf_op jit(solution)/shard_map/concatenate | solution.py:514
  15.4 83.7 %fused.1 = (f32[256,2048]{1,0:T(8,128)}, f32[256,1]{1,0:T(8,128)}, f32[64,2048]{1,0:T(8,128)}, f32[64,1]{1,0:T(8,128)}) custom-call(bf16[256,2048]{1,0:T(8,128)(2,1)} %query_ref.1, bf16[256,2048]{1,0:T(8,128)(2,1)} %key_ref.1, bf16[256,2048]{1,0:T(8,128)(2,1)} %value_ref.1, f32[16,256,6]{2,1,0:T(8,128)} %bitcast.41, f32[16,1,256]{2,1,0:T(1,128)} %bitcast.47, ...), custom_call_target="tpu_custom_call" | custom-call | tf_op jit(solution)/shard_map/fused/pallas_call | solution.py:412
  99.2 0.9 reduce.8
  100.1 1.0 reduce.7
  101.1 5.7 %all-reduce = (f32[256]{0:T(256)S(1)}, f32[64]{0:T(128)S(1)}) all-reduce(f32[256]{0:T(256)S(1)} %reduce.7, f32[64]{0:T(128)S(1)} %reduce.8), channel_id=1, replica_groups=mesh['seq'=8,'head'=4] {'head'}, use_global_device_ids=true, to_apply=%region_8.9 | all-reduce | flops 320 | bytes 2560 | tf_op jit(solution)/shard_map/psum | solution.py:561
  106.8 2.8 %multiply_convert_fusion = bf16[256,2048]{1,0:T(8,128)(2,1)} fusion(f32[256,2048]{1,0:T(8,128)} %get-tuple-element.6, f32[2048]{0:T(1024)S(1)} %copy-done.2, f32[256]{0:T(256)S(1)} %add_rsqrt_fusion), kind=kLoop, calls=%fused_computation | loop fusion | flops 1572864 | bytes 3154944 | tf_op jit(solution)/shard_map/convert_element_type | solution.py:565
  109.6 0.8 multiply_convert_fusion.1
  (27 shorter events, 0.8 us)
Async XLA Ops:
  0.6 10.1 %copy-start = (f32[4,16,16]{2,1,0:T(8,128)S(1)}, f32[4,16,16]{2,1,0:T(8,128)}, u32[]{:S(2)}) copy-start(f32[4,16,16]{2,1,0:T(8,128)} %param.21) | copy-start | bytes 12292
  15.4 91.4 %copy-start.2 = (f32[2048]{0:T(1024)S(1)}, f32[2048]{0:T(1024)}, u32[]{:S(2)}) copy-start(f32[2048]{0:T(1024)} %param.16) | copy-start | bytes 24580
  99.2 10.4 %copy-start.1 = (f32[64,2048]{1,0:T(8,128)S(1)}, f32[64,2048]{1,0:T(8,128)}, u32[]{:S(2)}) copy-start(f32[64,2048]{1,0:T(8,128)} %get-tuple-element.8) | copy-start | bytes 1572868

commit v4 on v3

--- a/solution.py
+++ b/solution.py
@@ -24,8 +24,7 @@
     query_ref,
     key_ref,
     value_ref,
-    cols_ref,
-    cum_ref,
+    token_ref,
     bias_ref,
     coef_ref,
     mask_ref,
@@ -147,8 +146,9 @@
     def make_parts(h, j, into):
         key = key_ref[:, lanes(h)].astype(f32)
         value = value_ref[:, lanes(h)]
+        cols = jnp.transpose(token_ref[h])
         for p in range(slots):
-            keyed = (key * cols_ref[h, :, p : p + 1]).astype(bf16)
+            keyed = (key * cols[:, p : p + 1]).astype(bf16)
             into[j, p] = lax.dot_general(
                 keyed, value, (((0,), (0,)), ((), ())), preferred_element_type=f32
             )
@@ -158,14 +158,15 @@
         scores = lax.dot_general(
             query, key_ref[:, lanes(h)], (((1,), (1,)), ((), ())), preferred_element_type=f32
         )
-        spread = cols_ref[h, :, slots : slots + 1] - cum_ref[h] + bias_ref[...]
+        cols = jnp.transpose(token_ref[h])
+        spread = cols[:, slots : slots + 1] - token_ref[h, slots : slots + 1, :] + bias_ref[...]
         weights = (scores * jnp.exp(spread)).astype(bf16)
         mixed_ref[:, lanes(h)] = jnp.dot(
             weights, value_ref[:, lanes(h)], preferred_element_type=f32
         )
 
     def across(h, entry):
-        carried = cols_ref[h, :, slots + 1 : slots + 2]
+        carried = jnp.transpose(token_ref[h])[:, slots + 1 : slots + 2]
         outer = jnp.dot(query_ref[:, lanes(h)], entry.astype(bf16), preferred_element_type=f32)
         mixed = mixed_ref[:, lanes(h)] + outer * carried
         mixed_ref[:, lanes(h)] = mixed
@@ -391,12 +392,21 @@
     def _():
         t_copy.wait_send()
 
-    square_ref[...] = jnp.sum(acc_sq[...], axis=1, keepdims=True)
-    dsquare_ref[...] = jnp.sum(acc_dsq[...], axis=1, keepdims=True)
+    def row_sums(acc):
+        return lax.dot_general(
+            jnp.ones((8, HDIM), f32),
+            acc[...],
+            (((1,), (1,)), ((), ())),
+            precision=lax.Precision.HIGHEST,
+            preferred_element_type=f32,
+        )
+
+    square_ref[...] = row_sums(acc_sq)
+    dsquare_ref[...] = row_sums(acc_dsq)
 
 
 def fused(n, steps, *operands):
-    query, coef, step = operands[0], operands[6], operands[8]
+    query, coef, step = operands[0], operands[5], operands[7]
     tok, width = query.shape
     heads, slots = coef.shape[:2]
     half = heads // PAIR
@@ -413,9 +423,9 @@
         functools.partial(fused_kernel, n, steps),
         out_shape=(
             jax.ShapeDtypeStruct((tok, width), f32),
-            jax.ShapeDtypeStruct((tok, 1), f32),
+            jax.ShapeDtypeStruct((8, tok), f32),
             jax.ShapeDtypeStruct((vectors, width), f32),
-            jax.ShapeDtypeStruct((vectors, 1), f32),
+            jax.ShapeDtypeStruct((8, vectors), f32),
         ),
         in_specs=[vmem] * len(operands),
         out_specs=(vmem,) * 4,
@@ -467,8 +477,13 @@
     )(*operands)
 
 
+def ends_of(prompt_lengths):
+    index = jnp.arange(prompt_lengths.shape[0])
+    return jnp.sum(jnp.where(index[:, None] >= index[None, :], prompt_lengths[None, :], 0), axis=1)
+
+
 def segment_ids(prompt_lengths, positions):
-    boundary = jnp.cumsum(prompt_lengths)
+    boundary = ends_of(prompt_lengths)
     return jnp.sum((positions[:, None] >= boundary[None, :]).astype(jnp.int32), axis=1)
 
 
@@ -493,7 +508,7 @@
     place = lax.axis_index("seq")
     first = place * tok
     pair_first = (place // PAIR) * (PAIR * tok)
-    ends = jnp.cumsum(prompt_lengths)
+    ends = ends_of(prompt_lengths)
     begins = ends - prompt_lengths
     segs = segment_ids(prompt_lengths, first + jnp.arange(tok, dtype=jnp.int32))
     slot = jnp.arange(PROMPTS, dtype=jnp.int32)
@@ -511,8 +526,8 @@
     taken = (segs[None, :] == slot[:, None])[:, :, None]
     keep = jnp.where(taken, jnp.exp(jnp.where(taken, reached[:, None, :] - cum[None], 0.0)), 0.0)
     carried = jnp.exp(cum) * (segs == seg_front).astype(f32)[:, None]
-    cols = jnp.transpose(jnp.concatenate([keep, cum[None], carried[None]]), (2, 1, 0))
-    cum_rows = cum.T[:, None, :]
+    spare = jnp.zeros_like(keep[:2])
+    tokens = jnp.transpose(jnp.concatenate([keep, cum[None], carried[None], spare]), (2, 0, 1))
     causal = jnp.arange(tok)[:, None] >= jnp.arange(tok)[None, :]
     linked = causal & (segs[:, None] == segs[None, :])
     bias = jnp.where(linked, 0.0, -jnp.inf)
@@ -547,8 +562,7 @@
         query_in,
         key_in,
         value_in,
-        cols,
-        cum_rows,
+        tokens,
         bias,
         coef,
         masks,
@@ -559,7 +573,7 @@
         row_marks,
     )
     squares, step_squares = lax.psum(
-        (mixed_sq[:, 0], decoded_sq[:, 0]), "head"
+        (mixed_sq[0], decoded_sq[0]), "head"
     )
     scale = lax.rsqrt(squares / (HEAD_COUNT * HDIM) + EPSILON)
     attn_out = (mixed * scale[:, None] * norm_gain[None, :]).astype(jnp.bfloat16)

time: 111 us -> 109 us (0.982)
  local copies, waits for them, and re-layouts: 6.64 us -> 5.37 us
    concatenate x1, local copies, waits for them, and re-layouts: 2.02 us -> 0.07 us  [local(): jnp.concatenate([keep, cum[None], carried[None], spare])]
    pallas_call x2 -> x0, other arithmetic: 1.94 us -> none  [fused(): pl.pallas_call(functools.partial(fused_kernel, n, steps), out_shape=(jax....]
    another operation x3 -> x1, local copies, waits for them, and re-layouts: 1.34 us -> 0.01 us
where the time goes in v4:
time: 109 us
  Pallas kernels  83.6 us (77%)
  other arithmetic  10.3 us (9%)
  blocking collectives  5.63 us (5%)
  local copies, waits for them, and re-layouts  5.37 us (5%)
  between operations  2.76 us (3%)
    pallas_call x1, Pallas kernels, fused(): pl.pallas_call(functools.partial(fused_kernel, n, steps), out_shape=(jax....  83.6 us
    psum x1, blocking collectives, local(): squares, step_squares = lax.psum((mixed_sq[0], decoded_sq[0]), 'head')  5.63 us
    convert_element_type x1, other arithmetic, local(): (mixed * scale[:, None] * norm_gain[None, :]).astype(jnp.bfloat16)  2.8 us

profile of v4, /device:TPU:0, one launch (start us, length us, event | category | flops | bytes accessed | tf_op | source)
XLA Modules:
  0.0 108.6 jit_solution(13579990990608442545)
XLA Ops:
  0.7 0.8 select_reduce_fusion.1
  1.4 0.7 fusion.5
  2.2 0.7 copy_bitcast_fusion
  2.9 0.6 reduce-window.6
  3.5 0.2 slice_reduce_fusion
  3.8 0.1 select_reduce_fusion
  3.9 0.1 convert_reduce_fusion
  4.0 0.1 exponential_select_fusion
  5.0 0.7 maximum_bitcast_fusion.token_ref
  5.7 0.7 broadcast_compare_fusion
  6.4 0.7 broadcast_in_dim.183.coef_ref
  8.5 0.7 broadcast_in_dim.184.mask_ref
  9.2 0.8 fusion.1.bias_ref
  10.0 1.0 fusion.2
  11.1 0.8 copy.34
  11.9 0.7 convert_element_type.50
  12.6 0.1 broadcast_in_dim.186
  12.7 0.7 broadcast_in_dim.187.row_ref
  13.3 83.6 %fused.1 = (f32[256,2048]{1,0:T(8,128)}, f32[8,256]{1,0:T(8,128)}, f32[64,2048]{1,0:T(8,128)}, f32[8,64]{1,0:T(8,128)}) custom-call(bf16[256,2048]{1,0:T(8,128)(2,1)} %query_ref.1, bf16[256,2048]{1,0:T(8,128)(2,1)} %key_ref.1, bf16[256,2048]{1,0:T(8,128)(2,1)} %value_ref.1, f32[16,8,256]{2,1,0:T(8,128)} %maximum_bitcast_fusion.token_ref, ...), custom_call_target="tpu_custom_call" | custom-call | tf_op jit(solution)/shard_map/fused/pallas_call | solution.py:422
  96.9 0.7 slice.14
  97.6 0.7 slice_bitcast_fusion
  98.3 5.6 %all-reduce = (f32[256]{0:T(256)S(1)}, f32[64]{0:T(128)S(1)}) all-reduce(f32[256]{0:T(256)S(1)} %bitcast.43, f32[64]{0:T(128)S(1)} %slice_bitcast_fusion), channel_id=1, replica_groups=mesh['seq'=8,'head'=4] {'head'}, use_global_device_ids=true, to_apply=%region_8.9 | all-reduce | flops 320 | bytes 2560 | tf_op jit(solution)/shard_map/psum | solution.py:575
  104.0 1.9 %multiply_convert_fusion.1 = bf16[64,2048]{1,0:T(8,128)(2,1)} fusion(f32[64,2048]{1,0:T(8,128)} %get-tuple-element.8, f32[2048]{0:T(1024)S(1)} %copy-done.1, f32[64]{0:T(128)S(1)} %add_rsqrt_fusion.1), kind=kLoop, calls=%fused_computation.1 | loop fusion | flops 393216 | bytes 794880 | tf_op jit(solution)/shard_map/convert_element_type | solution.py:581
  105.8 2.8 %multiply_convert_fusion = bf16[256,2048]{1,0:T(8,128)(2,1)} fusion(f32[256,2048]{1,0:T(8,128)} %get-tuple-element.6, f32[2048]{0:T(1024)S(1)} %copy-done.1, f32[256]{0:T(256)S(1)} %add_rsqrt_fusion), kind=kLoop, calls=%fused_computation | loop fusion | flops 1572864 | bytes 3154944 | tf_op jit(solution)/shard_map/convert_element_type | solution.py:579
  (24 shorter events, 0.6 us)
Async XLA Ops:
  0.6 9.4 %copy-start = (f32[4,16,16]{2,1,0:T(8,128)S(1)}, f32[4,16,16]{2,1,0:T(8,128)}, u32[]{:S(2)}) copy-start(f32[4,16,16]{2,1,0:T(8,128)} %param.21) | copy-start | bytes 12292
  13.3 90.6 %copy-start.1 = (f32[2048]{0:T(1024)S(1)}, f32[2048]{0:T(1024)}, u32[]{:S(2)}) copy-start(f32[2048]{0:T(1024)} %param.16) | copy-start | bytes 24580
